TPU v7x, 128 devices: a whole 4x4x4 slice. The times are simulated.
128 devices in a mesh: blk: 16 (over y_lo, x, core), group: 8 (over z, y_hi).
Axes of the slice: x: 4, y: 4 (y_hi: 2, y_lo: 2; y = y_hi * 2 + y_lo), z: 4, core: 2. Of those that a mesh axis runs over, the one named last changes fastest.
Arguments:
- image_embed: bfloat16 [8192, 1152], P(('blk', 'group')), may hold values from -6 to 6
- caption_vectors: bfloat16 [65536, 1152], P(('blk', 'group')), may hold values from -6 to 6
- caption_counts: int32 [8192], replicated, may hold values from 1 to 8, as said below
- natural_log_multiplier: float32 [1], replicated, may hold values from 1.5 to 2.5
- match_odds_offset: float32 [1], replicated, may hold values from -6 to -4
Outputs:
- image_grad: float32 [8192, 1152], P(('blk', 'group'))
- caption_grad: float32 [65536, 1152], P(('blk', 'group'))
Inputs may be any that keep to these rules, and one draw needn't show every extreme that they name: Images are numbered as in caption_counts, 64 to a device, devices in the order of blk then group. Local image k of the device with blk index b < 8 and group index g and local image k of the device with blk index b + 8 and group index g have counts that sum to 9. On at least one device all 64 images have 8 captions.
All inputs are finite; a program needn't handle non-finite values.
Results may differ from a plain program's by a relative error of at most 0.0028.
Values may be sent and summed in bfloat16 or wider, within the bound.
A program may use at most 64 MiB of HBM per device.

v0:
```python
import jax
import jax.numpy as jnp
from jax import lax
from jax.sharding import PartitionSpec as P

EPSILON = 1e-06


def swapped(value, axis, stride):
    return lax.ppermute(value, axis, [(i, i ^ 1 << stride) for i in range(lax.axis_size(axis))])


def shifted(block, axis, distance):
    devices = range(lax.axis_size(axis))
    route = [((i - distance) % len(devices), i) for i in devices]
    return lax.ppermute(block, axis, route)


def normalize(embed_rows):
    values = embed_rows.astype(jnp.float32)
    inverse = lax.rsqrt(jnp.sum(values * values, axis=1, keepdims=True) + EPSILON)
    return (values * inverse, inverse)


def slot_owners(device_counts, first_image, slot_count):
    running_end = jnp.cumsum(device_counts)
    position = lax.broadcasted_iota(jnp.int32, (slot_count, device_counts.shape[0]), 0)
    local_index = jnp.sum((running_end[None, :] <= position).astype(jnp.int32), axis=1)
    present_entry_flags = position[:, 0] < running_end[-1]
    return jnp.where(present_entry_flags, first_image + local_index, -1)


def balanced_pick(own_total, slot_count, kept_rows):
    position = lax.iota(jnp.int32, kept_rows)
    return jnp.where(position < own_total, position, slot_count + position - own_total)


def shards(image_embed, caption_vectors, caption_counts, natural_log_multiplier, match_odds_offset):
    image_count = image_embed.shape[0]
    slot_count = caption_vectors.shape[0]
    kept_rows = 9 * image_count // 2
    blocks = lax.axis_size("blk")
    groups = lax.axis_size("group")
    pair_bit = blocks.bit_length() - 2
    blk_index = lax.axis_index("blk")
    group_index = lax.axis_index("group")
    odds_sharpness_factor = jnp.exp(natural_log_multiplier[0])
    bias_value = match_odds_offset[0]
    image_unit, image_inverse = normalize(image_embed)
    caption_unit, caption_inverse = normalize(caption_vectors)
    caption_low = caption_unit.astype(jnp.bfloat16)
    gathered = lax.all_gather(image_unit.astype(jnp.bfloat16), "blk", axis=0, tiled=True)
    column_pos = lax.iota(jnp.int32, blocks * image_count)
    column_ids = (
        column_pos // image_count * groups + group_index
    ) * image_count + column_pos % image_count

    def device_counts(device_id):
        return lax.dynamic_slice_in_dim(caption_counts, device_id * image_count, image_count)

    def source_owners(source_group):
        own_id = blk_index * groups + source_group
        own_counts = device_counts(own_id)
        own_owner = slot_owners(own_counts, own_id * image_count, slot_count)
        partner_id = (blk_index ^ blocks // 2) * groups + source_group
        partner_owner = slot_owners(device_counts(partner_id), partner_id * image_count, slot_count)
        own_total = jnp.sum(own_counts)
        joined = jnp.concatenate([own_owner, partner_owner[kept_rows:]])
        return jnp.take(joined, balanced_pick(own_total, slot_count, kept_rows))

    owner_table = jax.vmap(source_owners)(lax.iota(jnp.int32, groups))
    home_id = blk_index * groups + group_index
    home_counts = device_counts(home_id)
    home_total = jnp.sum(home_counts)
    home_owner = slot_owners(home_counts, home_id * image_count, slot_count)
    partner_tail = swapped(caption_low[kept_rows:], "blk", pair_bit)
    moving_rows = jnp.take(
        jnp.concatenate([caption_low, partner_tail], axis=0),
        balanced_pick(home_total, slot_count, kept_rows),
        axis=0,
    )

    def row_terms(moving, grad_rows, owners, image_acc):
        similarity_matrix = (
            odds_sharpness_factor
            * lax.dot_general(
                moving, gathered, (((1,), (1,)), ((), ())), preferred_element_type=jnp.float32
            )
            + bias_value
        )
        match_target_signs = jnp.where(owners[:, None] == column_ids[None, :], 1.0, -1.0)
        present_entry_flags = (owners >= 0)[:, None]
        oriented_similarity_gap = match_target_signs * similarity_matrix
        match_loss_factors = jnp.where(
            present_entry_flags,
            odds_sharpness_factor
            * (-match_target_signs * jax.nn.sigmoid(-oriented_similarity_gap)),
            0.0,
        ).astype(jnp.bfloat16)
        grad_rows = grad_rows + jnp.dot(
            match_loss_factors, gathered, preferred_element_type=jnp.float32
        )
        image_acc = image_acc + lax.dot_general(
            match_loss_factors, moving, (((0,), (0,)), ((), ())), preferred_element_type=jnp.float32
        )
        return (grad_rows, image_acc)

    def owners_from(source_group):
        return lax.dynamic_index_in_dim(owner_table, source_group % groups, 0, keepdims=False)

    row_count = moving_rows.shape[0]
    image_acc = jnp.zeros(gathered.shape, jnp.float32)
    half_rows = row_count // 2

    def pass_both(ahead_grad, behind_grad):
        ahead_grad = shifted(ahead_grad, "group", 1)
        behind_grad = shifted(behind_grad, "group", -1)
        return (ahead_grad, behind_grad)

    def both_terms(step_index, ahead, behind, ahead_grad, behind_grad, image_acc):
        ahead_owner = owners_from(group_index - step_index)[:half_rows]
        behind_owner = owners_from(group_index + step_index)[half_rows:]
        ahead_grad, image_acc = row_terms(ahead, ahead_grad, ahead_owner, image_acc)
        behind_grad, image_acc = row_terms(behind, behind_grad, behind_owner, image_acc)
        return (ahead_grad, behind_grad, image_acc)

    ahead_start = moving_rows[:half_rows]
    behind_start = moving_rows[half_rows:]
    zero_half = jnp.zeros((half_rows, gathered.shape[1]), jnp.float32)
    ahead_grad, behind_grad, image_acc = both_terms(
        0, ahead_start, behind_start, zero_half, zero_half, image_acc
    )

    def turn_both(step_index, loop_state):
        ahead, behind, ahead_grad, behind_grad, image_acc = loop_state
        ahead = shifted(ahead, "group", 1)
        behind = shifted(behind, "group", -1)
        ahead_grad, behind_grad = pass_both(ahead_grad, behind_grad)
        ahead_grad, behind_grad, image_acc = both_terms(
            step_index, ahead, behind, ahead_grad, behind_grad, image_acc
        )
        return (ahead, behind, ahead_grad, behind_grad, image_acc)

    loop_state = lax.fori_loop(
        1, groups, turn_both, (ahead_start, behind_start, ahead_grad, behind_grad, image_acc)
    )
    ahead_grad, behind_grad = pass_both(loop_state[2], loop_state[3])
    grad_total = jnp.concatenate([ahead_grad, behind_grad], axis=0)
    image_acc = loop_state[4]
    image_sum = lax.psum_scatter(image_acc, "blk", scatter_dimension=0, tiled=True)
    image_grad = (
        image_sum - image_unit * jnp.sum(image_unit * image_sum, axis=1, keepdims=True)
    ) * image_inverse
    back_pos = home_total + lax.iota(jnp.int32, slot_count - kept_rows)
    back_rows = jnp.where(
        (back_pos < kept_rows)[:, None],
        jnp.take(grad_total, jnp.minimum(back_pos, kept_rows - 1), axis=0),
        0.0,
    )
    returned = swapped(back_rows, "blk", pair_bit)
    head_rows = jnp.where((lax.iota(jnp.int32, kept_rows) < home_total)[:, None], grad_total, 0.0)
    slot_grads = jnp.concatenate([head_rows, returned], axis=0)
    caption_grad = jnp.where(
        (home_owner >= 0)[:, None],
        (slot_grads - caption_unit * jnp.sum(caption_unit * slot_grads, axis=1, keepdims=True))
        * caption_inverse,
        0.0,
    )
    return (image_grad, caption_grad)


def solution(mesh):
    placed = (P(("blk", "group"), None), P(("blk", "group"), None), P(), P(), P())
    return jax.shard_map(
        shards,
        mesh=mesh,
        in_specs=placed,
        out_specs=(P(("blk", "group"), None), P(("blk", "group"), None)),
        check_vma=False,
    )
```

profile of v0, /device:TPU:1, one launch (start us, length us, event | category | flops | bytes accessed | tf_op | source)
XLA Modules:
  0.0 499.8 jit_solution(15100584255901082018)
XLA Ops:
  13.7 15.7 %while.27 = (s32[]{:T(128)}, s32[8192]{0:T(1024)}, s32[8,1]{0,1:T(1,128)S(1)}, s32[8,64]{1,0:T(8,128)S(1)}, s32[]{:T(128)}, /*index=5*/s32[]{:T(128)}) while((s32[]{:T(128)}, s32[8192]{0:T(1024)}, s32[8,1]{0,1:T(1,128)S(1)}, s32[8,64]{1,0:T(8,128)S(1)}, s32[]{:T(128)}, /*index=5*/s32[]{:T(128)}) %tuple.78), condition=%wide.while_cond, body=%wide.while_body.sunk | while | flops 2 | bytes 1113 | solution.py:59
  30.0 16.2 %while.28 = (s32[]{:T(128)}, s32[8192]{0:T(1024)}, s32[8,1]{0,1:T(1,128)S(1)}, s32[8,64]{1,0:T(8,128)S(1)}, s32[]{:T(128)}, /*index=5*/s32[]{:T(128)}) while((s32[]{:T(128)}, s32[8192]{0:T(1024)}, s32[8,1]{0,1:T(1,128)S(1)}, s32[8,64]{1,0:T(8,128)S(1)}, s32[]{:T(128)}, /*index=5*/s32[]{:T(128)}) %tuple.89), condition=%wide.while_cond.1, body=%wide.while_body.1.sunk | while | flops 2 | bytes 1113 | solution.py:59
  47.4 13.6 %gather_fusion.2 = s32[2304]{0:T(1024)S(1)} fusion(s32[8,736]{1,0:T(8,128)S(1)} %pad_add_fusion, s32[2304]{0:T(1024)S(1)} %reshape.382), kind=kCustom, calls=%fused_computation.2 | custom fusion | bytes 36864 | tf_op jit(solution)/shard_map/vmap(jit(_take))/gather | solution.py:69
  79.8 333.8 %while.29 = (s32[]{:T(128)}, bf16[144,1152]{1,0:T(8,128)(2,1)}, bf16[144,1152]{1,0:T(8,128)(2,1)S(1)}, f32[144,1152]{1,0:T(8,128)}, f32[144,1152]{1,0:T(8,128)},...) while((s32[]{:T(128)}, bf16[144,1152]{1,0:T(8,128)(2,1)}, ...), condition=%wide.region_9.10_spmd.clone.clone, body=%wide.region_8.9_spmd.clone.clone.sunk | while | flops 2044678400 | bytes 76400416 | solution.py:144
  79.8 6.1 %collective-permute-start.1 = (bf16[144,1152]{1,0:T(8,128)(2,1)S(1)}, bf16[144,1152]{1,0:T(8,128)(2,1)S(1)}, u32[]{:S(2)}, u32[]{:S(2)}) collective-permute-start(bf16[144,1152]{1,0:T(8,128)(2,1)S(1)} %get-tuple-element.586), channel_id=1, source_target_pairs={{1,0},{2,1},{3,2},{4,3},{5,4},{6,5},{7,6},{0,7},{9,8},{10,9},{11,1... | collective-permute-start | bytes 995336 | tf_op jit(solution)/shard_map/while/body/eval_jaxpr/ppermute | solution.py:16
  104.6 10.0 %collective-permute-done.2 = f32[144,1152]{1,0:T(8,128)} collective-permute-done((f32[144,1152]{1,0:T(8,128)}, f32[144,1152]{1,0:T(8,128)}, u32[]{:S(2)}, u32[]{:S(2)}) %collective-permute-start.2) | collective-permute-done | bytes 663584 | tf_op jit(solution)/shard_map/while/body/eval_jaxpr/ppermute | solution.py:16
  117.1 10.7 %collective-permute-done.3 = f32[144,1152]{1,0:T(8,128)} collective-permute-done((f32[144,1152]{1,0:T(8,128)}, f32[144,1152]{1,0:T(8,128)}, u32[]{:S(2)}, u32[]{:S(2)}) %collective-permute-start.3) | collective-permute-done | bytes 663584 | tf_op jit(solution)/shard_map/while/body/eval_jaxpr/ppermute | solution.py:16
  154.1 10.0 %collective-permute-done.2 = f32[144,1152]{1,0:T(8,128)} collective-permute-done((f32[144,1152]{1,0:T(8,128)}, f32[144,1152]{1,0:T(8,128)}, u32[]{:S(2)}, u32[]{:S(2)}) %collective-permute-start.2) | collective-permute-done | bytes 663584 | tf_op jit(solution)/shard_map/while/body/eval_jaxpr/ppermute | solution.py:16
  166.5 10.6 %collective-permute-done.3 = f32[144,1152]{1,0:T(8,128)} collective-permute-done((f32[144,1152]{1,0:T(8,128)}, f32[144,1152]{1,0:T(8,128)}, u32[]{:S(2)}, u32[]{:S(2)}) %collective-permute-start.3) | collective-permute-done | bytes 663584 | tf_op jit(solution)/shard_map/while/body/eval_jaxpr/ppermute | solution.py:16
  203.4 10.0 %collective-permute-done.2 = f32[144,1152]{1,0:T(8,128)} collective-permute-done((f32[144,1152]{1,0:T(8,128)}, f32[144,1152]{1,0:T(8,128)}, u32[]{:S(2)}, u32[]{:S(2)}) %collective-permute-start.2) | collective-permute-done | bytes 663584 | tf_op jit(solution)/shard_map/while/body/eval_jaxpr/ppermute | solution.py:16
  215.9 9.7 %collective-permute-done.3 = f32[144,1152]{1,0:T(8,128)} collective-permute-done((f32[144,1152]{1,0:T(8,128)}, f32[144,1152]{1,0:T(8,128)}, u32[]{:S(2)}, u32[]{:S(2)}) %collective-permute-start.3) | collective-permute-done | bytes 663584 | tf_op jit(solution)/shard_map/while/body/eval_jaxpr/ppermute | solution.py:16
  251.6 10.0 %collective-permute-done.2 = f32[144,1152]{1,0:T(8,128)} collective-permute-done((f32[144,1152]{1,0:T(8,128)}, f32[144,1152]{1,0:T(8,128)}, u32[]{:S(2)}, u32[]{:S(2)}) %collective-permute-start.2) | collective-permute-done | bytes 663584 | tf_op jit(solution)/shard_map/while/body/eval_jaxpr/ppermute | solution.py:16
  264.1 9.2 %collective-permute-done.3 = f32[144,1152]{1,0:T(8,128)} collective-permute-done((f32[144,1152]{1,0:T(8,128)}, f32[144,1152]{1,0:T(8,128)}, u32[]{:S(2)}, u32[]{:S(2)}) %collective-permute-start.3) | collective-permute-done | bytes 663584 | tf_op jit(solution)/shard_map/while/body/eval_jaxpr/ppermute | solution.py:16
  289.4 5.8 %collective-permute-done = bf16[144,1152]{1,0:T(8,128)(2,1)S(1)} collective-permute-done((bf16[144,1152]{1,0:T(8,128)(2,1)}, bf16[144,1152]{1,0:T(8,128)(2,1)S(1)}, u32[]{:S(2)}, u32[]{:S(2)}) %collective-permute-start) | collective-permute-done | bytes 331808 | tf_op jit(solution)/shard_map/while/body/eval_jaxpr/ppermute | solution.py:16
  299.6 10.0 %collective-permute-done.2 = f32[144,1152]{1,0:T(8,128)} collective-permute-done((f32[144,1152]{1,0:T(8,128)}, f32[144,1152]{1,0:T(8,128)}, u32[]{:S(2)}, u32[]{:S(2)}) %collective-permute-start.2) | collective-permute-done | bytes 663584 | tf_op jit(solution)/shard_map/while/body/eval_jaxpr/ppermute | solution.py:16
  312.1 8.0 %collective-permute-done.3 = f32[144,1152]{1,0:T(8,128)} collective-permute-done((f32[144,1152]{1,0:T(8,128)}, f32[144,1152]{1,0:T(8,128)}, u32[]{:S(2)}, u32[]{:S(2)}) %collective-permute-start.3) | collective-permute-done | bytes 663584 | tf_op jit(solution)/shard_map/while/body/eval_jaxpr/ppermute | solution.py:16
  346.0 10.3 %collective-permute-done.2 = f32[144,1152]{1,0:T(8,128)} collective-permute-done((f32[144,1152]{1,0:T(8,128)}, f32[144,1152]{1,0:T(8,128)}, u32[]{:S(2)}, u32[]{:S(2)}) %collective-permute-start.2) | collective-permute-done | bytes 663584 | tf_op jit(solution)/shard_map/while/body/eval_jaxpr/ppermute | solution.py:16
  358.7 7.2 %collective-permute-done.3 = f32[144,1152]{1,0:T(8,128)} collective-permute-done((f32[144,1152]{1,0:T(8,128)}, f32[144,1152]{1,0:T(8,128)}, u32[]{:S(2)}, u32[]{:S(2)}) %collective-permute-start.3) | collective-permute-done | bytes 663584 | tf_op jit(solution)/shard_map/while/body/eval_jaxpr/ppermute | solution.py:16
  391.1 10.3 %collective-permute-done.2 = f32[144,1152]{1,0:T(8,128)} collective-permute-done((f32[144,1152]{1,0:T(8,128)}, f32[144,1152]{1,0:T(8,128)}, u32[]{:S(2)}, u32[]{:S(2)}) %collective-permute-start.2) | collective-permute-done | bytes 663584 | tf_op jit(solution)/shard_map/while/body/eval_jaxpr/ppermute | solution.py:16
  403.8 7.2 %collective-permute-done.3 = f32[144,1152]{1,0:T(8,128)} collective-permute-done((f32[144,1152]{1,0:T(8,128)}, f32[144,1152]{1,0:T(8,128)}, u32[]{:S(2)}, u32[]{:S(2)}) %collective-permute-start.3) | collective-permute-done | bytes 663584 | tf_op jit(solution)/shard_map/while/body/eval_jaxpr/ppermute | solution.py:16
  422.4 6.1 %collective-permute-done.5 = f32[144,1152]{1,0:T(8,128)S(1)} collective-permute-done((f32[144,1152]{1,0:T(8,128)S(1)}, f32[144,1152]{1,0:T(8,128)S(1)}, u32[]{:S(2)}, u32[]{:S(2)}) %collective-permute-start.5) | collective-permute-done | bytes 663584 | tf_op jit(solution)/shard_map/ppermute | solution.py:16
  428.6 15.6 %collective-permute-done.6 = f32[144,1152]{1,0:T(8,128)S(1)} collective-permute-done((f32[144,1152]{1,0:T(8,128)S(1)}, f32[144,1152]{1,0:T(8,128)S(1)}, u32[]{:S(2)}, u32[]{:S(2)}) %collective-permute-start.6) | collective-permute-done | bytes 663584 | tf_op jit(solution)/shard_map/ppermute | solution.py:16
  453.1 27.0 %collective-permute-done.7 = f32[224,1152]{1,0:T(8,128)S(1)} collective-permute-done((f32[224,1152]{1,0:T(8,128)}, f32[224,1152]{1,0:T(8,128)S(1)}, u32[]{:S(2)}, u32[]{:S(2)}) %collective-permute-start.7) | collective-permute-done | bytes 1032224 | tf_op jit(solution)/shard_map/ppermute | solution.py:10
  482.5 7.4 %reduce-scatter.2.cloned.1.call-done = f32[64,1152]{1,0:T(8,128)} async-done(((f32[1024,1152]{1,0:T(8,128)}), f32[64,1152]{1,0:T(8,128)}) %reduce-scatter.2.cloned.1.call-update) | async-done | bytes 294928 | tf_op jit(solution)/shard_map/reduce_scatter | solution.py:150
  (311 shorter events, 269.0 us)
Async XLA Ops:
  7.2 61.3 %all-gather.2.cloned.1.call-start = ((), (), s32[]{:S(2)}) async-start(), calls=%async_computation.1 | async-start | bytes 2506752 | tf_op jit(solution)/shard_map/all_gather | solution.py:52
  10.4 54.8 %collective-permute-start.4 = (bf16[224,1152]{1,0:T(8,128)(2,1)S(1)}, bf16[224,1152]{1,0:T(8,128)(2,1)S(1)}, u32[]{:S(2)}, u32[]{:S(2)}) collective-permute-start(bf16[224,1152]{1,0:T(8,128)(2,1)S(1)} %slice.107), channel_id=1, source_target_pairs={{0,64},{8,72},{16,80},{24,88},{32,96},{40,104},{48,112},{56,120},{... | collective-permute-start | bytes 1548296 | tf_op jit(solution)/shard_map/ppermute | solution.py:10
  13.5 476.4 %reduce-scatter.2.cloned.1.call-start = ((), (), s32[]{:S(2)}) async-start(), calls=%async_computation.2 | async-start | bytes 5013504 | tf_op jit(solution)/shard_map/reduce_scatter | solution.py:150
  85.9 14.4 %collective-permute-start = (bf16[144,1152]{1,0:T(8,128)(2,1)}, bf16[144,1152]{1,0:T(8,128)(2,1)S(1)}, u32[]{:S(2)}, u32[]{:S(2)}) collective-permute-start(bf16[144,1152]{1,0:T(8,128)(2,1)} %get-tuple-element.585), channel_id=1, source_target_pairs={{7,0},{0,1},{1,2},{2,3},{3,4},{4,5},{5,6},{6,7},{15,8},{8,9},{9,10... | collective-permute-start | bytes 995336 | tf_op jit(solution)/shard_map/while/body/eval_jaxpr/ppermute | solution.py:16
  85.9 28.7 %collective-permute-start.2 = (f32[144,1152]{1,0:T(8,128)}, f32[144,1152]{1,0:T(8,128)}, u32[]{:S(2)}, u32[]{:S(2)}) collective-permute-start(f32[144,1152]{1,0:T(8,128)} %get-tuple-element.587), channel_id=1, source_target_pairs={{7,0},{0,1},{1,2},{2,3},{3,4},{4,5},{5,6},{6,7},{15,8},{8,9},{9,10... | collective-permute-start | bytes 1990664 | tf_op jit(solution)/shard_map/while/body/eval_jaxpr/ppermute | solution.py:16
  86.3 41.5 %collective-permute-start.3 = (f32[144,1152]{1,0:T(8,128)}, f32[144,1152]{1,0:T(8,128)}, u32[]{:S(2)}, u32[]{:S(2)}) collective-permute-start(f32[144,1152]{1,0:T(8,128)} %get-tuple-element.588), channel_id=1, source_target_pairs={{1,0},{2,1},{3,2},{4,3},{5,4},{6,5},{7,6},{0,7},{9,8},{10,9},{11,1... | collective-permute-start | bytes 1990664 | tf_op jit(solution)/shard_map/while/body/eval_jaxpr/ppermute | solution.py:16
  136.1 13.6 %collective-permute-start = (bf16[144,1152]{1,0:T(8,128)(2,1)}, bf16[144,1152]{1,0:T(8,128)(2,1)S(1)}, u32[]{:S(2)}, u32[]{:S(2)}) collective-permute-start(bf16[144,1152]{1,0:T(8,128)(2,1)} %get-tuple-element.585), channel_id=1, source_target_pairs={{7,0},{0,1},{1,2},{2,3},{3,4},{4,5},{5,6},{6,7},{15,8},{8,9},{9,10... | collective-permute-start | bytes 995336 | tf_op jit(solution)/shard_map/while/body/eval_jaxpr/ppermute | solution.py:16
  136.1 28.0 %collective-permute-start.2 = (f32[144,1152]{1,0:T(8,128)}, f32[144,1152]{1,0:T(8,128)}, u32[]{:S(2)}, u32[]{:S(2)}) collective-permute-start(f32[144,1152]{1,0:T(8,128)} %get-tuple-element.587), channel_id=1, source_target_pairs={{7,0},{0,1},{1,2},{2,3},{3,4},{4,5},{5,6},{6,7},{15,8},{8,9},{9,10... | collective-permute-start | bytes 1990664 | tf_op jit(solution)/shard_map/while/body/eval_jaxpr/ppermute | solution.py:16
  136.1 41.0 %collective-permute-start.3 = (f32[144,1152]{1,0:T(8,128)}, f32[144,1152]{1,0:T(8,128)}, u32[]{:S(2)}, u32[]{:S(2)}) collective-permute-start(f32[144,1152]{1,0:T(8,128)} %get-tuple-element.588), channel_id=1, source_target_pairs={{1,0},{2,1},{3,2},{4,3},{5,4},{6,5},{7,6},{0,7},{9,8},{10,9},{11,1... | collective-permute-start | bytes 1990664 | tf_op jit(solution)/shard_map/while/body/eval_jaxpr/ppermute | solution.py:16
  185.4 13.6 %collective-permute-start = (bf16[144,1152]{1,0:T(8,128)(2,1)}, bf16[144,1152]{1,0:T(8,128)(2,1)S(1)}, u32[]{:S(2)}, u32[]{:S(2)}) collective-permute-start(bf16[144,1152]{1,0:T(8,128)(2,1)} %get-tuple-element.585), channel_id=1, source_target_pairs={{7,0},{0,1},{1,2},{2,3},{3,4},{4,5},{5,6},{6,7},{15,8},{8,9},{9,10... | collective-permute-start | bytes 995336 | tf_op jit(solution)/shard_map/while/body/eval_jaxpr/ppermute | solution.py:16
  185.4 28.0 %collective-permute-start.2 = (f32[144,1152]{1,0:T(8,128)}, f32[144,1152]{1,0:T(8,128)}, u32[]{:S(2)}, u32[]{:S(2)}) collective-permute-start(f32[144,1152]{1,0:T(8,128)} %get-tuple-element.587), channel_id=1, source_target_pairs={{7,0},{0,1},{1,2},{2,3},{3,4},{4,5},{5,6},{6,7},{15,8},{8,9},{9,10... | collective-permute-start | bytes 1990664 | tf_op jit(solution)/shard_map/while/body/eval_jaxpr/ppermute | solution.py:16
  185.4 40.1 %collective-permute-start.3 = (f32[144,1152]{1,0:T(8,128)}, f32[144,1152]{1,0:T(8,128)}, u32[]{:S(2)}, u32[]{:S(2)}) collective-permute-start(f32[144,1152]{1,0:T(8,128)} %get-tuple-element.588), channel_id=1, source_target_pairs={{1,0},{2,1},{3,2},{4,3},{5,4},{6,5},{7,6},{0,7},{9,8},{10,9},{11,1... | collective-permute-start | bytes 1990664 | tf_op jit(solution)/shard_map/while/body/eval_jaxpr/ppermute | solution.py:16
  233.9 27.6 %collective-permute-start.2 = (f32[144,1152]{1,0:T(8,128)}, f32[144,1152]{1,0:T(8,128)}, u32[]{:S(2)}, u32[]{:S(2)}) collective-permute-start(f32[144,1152]{1,0:T(8,128)} %get-tuple-element.587), channel_id=1, source_target_pairs={{7,0},{0,1},{1,2},{2,3},{3,4},{4,5},{5,6},{6,7},{15,8},{8,9},{9,10... | collective-permute-start | bytes 1990664 | tf_op jit(solution)/shard_map/while/body/eval_jaxpr/ppermute | solution.py:16
  233.9 39.3 %collective-permute-start.3 = (f32[144,1152]{1,0:T(8,128)}, f32[144,1152]{1,0:T(8,128)}, u32[]{:S(2)}, u32[]{:S(2)}) collective-permute-start(f32[144,1152]{1,0:T(8,128)} %get-tuple-element.588), channel_id=1, source_target_pairs={{1,0},{2,1},{3,2},{4,3},{5,4},{6,5},{7,6},{0,7},{9,8},{10,9},{11,1... | collective-permute-start | bytes 1990664 | tf_op jit(solution)/shard_map/while/body/eval_jaxpr/ppermute | solution.py:16
  281.6 13.6 %collective-permute-start = (bf16[144,1152]{1,0:T(8,128)(2,1)}, bf16[144,1152]{1,0:T(8,128)(2,1)S(1)}, u32[]{:S(2)}, u32[]{:S(2)}) collective-permute-start(bf16[144,1152]{1,0:T(8,128)(2,1)} %get-tuple-element.585), channel_id=1, source_target_pairs={{7,0},{0,1},{1,2},{2,3},{3,4},{4,5},{5,6},{6,7},{15,8},{8,9},{9,10... | collective-permute-start | bytes 995336 | tf_op jit(solution)/shard_map/while/body/eval_jaxpr/ppermute | solution.py:16
  281.6 28.0 %collective-permute-start.2 = (f32[144,1152]{1,0:T(8,128)}, f32[144,1152]{1,0:T(8,128)}, u32[]{:S(2)}, u32[]{:S(2)}) collective-permute-start(f32[144,1152]{1,0:T(8,128)} %get-tuple-element.587), channel_id=1, source_target_pairs={{7,0},{0,1},{1,2},{2,3},{3,4},{4,5},{5,6},{6,7},{15,8},{8,9},{9,10... | collective-permute-start | bytes 1990664 | tf_op jit(solution)/shard_map/while/body/eval_jaxpr/ppermute | solution.py:16
  281.6 38.4 %collective-permute-start.3 = (f32[144,1152]{1,0:T(8,128)}, f32[144,1152]{1,0:T(8,128)}, u32[]{:S(2)}, u32[]{:S(2)}) collective-permute-start(f32[144,1152]{1,0:T(8,128)} %get-tuple-element.588), channel_id=1, source_target_pairs={{1,0},{2,1},{3,2},{4,3},{5,4},{6,5},{7,6},{0,7},{9,8},{10,9},{11,1... | collective-permute-start | bytes 1990664 | tf_op jit(solution)/shard_map/while/body/eval_jaxpr/ppermute | solution.py:16
  328.4 27.8 %collective-permute-start.2 = (f32[144,1152]{1,0:T(8,128)}, f32[144,1152]{1,0:T(8,128)}, u32[]{:S(2)}, u32[]{:S(2)}) collective-permute-start(f32[144,1152]{1,0:T(8,128)} %get-tuple-element.587), channel_id=1, source_target_pairs={{7,0},{0,1},{1,2},{2,3},{3,4},{4,5},{5,6},{6,7},{15,8},{8,9},{9,10... | collective-permute-start | bytes 1990664 | tf_op jit(solution)/shard_map/while/body/eval_jaxpr/ppermute | solution.py:16
  328.4 37.6 %collective-permute-start.3 = (f32[144,1152]{1,0:T(8,128)}, f32[144,1152]{1,0:T(8,128)}, u32[]{:S(2)}, u32[]{:S(2)}) collective-permute-start(f32[144,1152]{1,0:T(8,128)} %get-tuple-element.588), channel_id=1, source_target_pairs={{1,0},{2,1},{3,2},{4,3},{5,4},{6,5},{7,6},{0,7},{9,8},{10,9},{11,1... | collective-permute-start | bytes 1990664 | tf_op jit(solution)/shard_map/while/body/eval_jaxpr/ppermute | solution.py:16
  374.3 27.0 %collective-permute-start.2 = (f32[144,1152]{1,0:T(8,128)}, f32[144,1152]{1,0:T(8,128)}, u32[]{:S(2)}, u32[]{:S(2)}) collective-permute-start(f32[144,1152]{1,0:T(8,128)} %get-tuple-element.587), channel_id=1, source_target_pairs={{7,0},{0,1},{1,2},{2,3},{3,4},{4,5},{5,6},{6,7},{15,8},{8,9},{9,10... | collective-permute-start | bytes 1990664 | tf_op jit(solution)/shard_map/while/body/eval_jaxpr/ppermute | solution.py:16
  374.3 36.7 %collective-permute-start.3 = (f32[144,1152]{1,0:T(8,128)}, f32[144,1152]{1,0:T(8,128)}, u32[]{:S(2)}, u32[]{:S(2)}) collective-permute-start(f32[144,1152]{1,0:T(8,128)} %get-tuple-element.588), channel_id=1, source_target_pairs={{1,0},{2,1},{3,2},{4,3},{5,4},{6,5},{7,6},{0,7},{9,8},{10,9},{11,1... | collective-permute-start | bytes 1990664 | tf_op jit(solution)/shard_map/while/body/eval_jaxpr/ppermute | solution.py:16
  414.7 13.9 %collective-permute-start.5 = (f32[144,1152]{1,0:T(8,128)S(1)}, f32[144,1152]{1,0:T(8,128)S(1)}, u32[]{:S(2)}, u32[]{:S(2)}) collective-permute-start(f32[144,1152]{1,0:T(8,128)S(1)} %copy-done.6), channel_id=1, source_target_pairs={{7,0},{0,1},{1,2},{2,3},{3,4},{4,5},{5,6},{6,7},{15,8},{8,9},{9,10... | collective-permute-start | bytes 1990664 | tf_op jit(solution)/shard_map/ppermute | solution.py:16
  414.9 29.3 %collective-permute-start.6 = (f32[144,1152]{1,0:T(8,128)S(1)}, f32[144,1152]{1,0:T(8,128)S(1)}, u32[]{:S(2)}, u32[]{:S(2)}) collective-permute-start(f32[144,1152]{1,0:T(8,128)S(1)} %copy-done.5), channel_id=1, source_target_pairs={{1,0},{2,1},{3,2},{4,3},{5,4},{6,5},{7,6},{0,7},{9,8},{10,9},{11,1... | collective-permute-start | bytes 1990664 | tf_op jit(solution)/shard_map/ppermute | solution.py:16
  447.3 32.8 %collective-permute-start.7 = (f32[224,1152]{1,0:T(8,128)}, f32[224,1152]{1,0:T(8,128)S(1)}, u32[]{:S(2)}, u32[]{:S(2)}) collective-permute-start(f32[224,1152]{1,0:T(8,128)} %select_select_fusion), channel_id=1, source_target_pairs={{0,64},{8,72},{16,80},{24,88},{32,96},{40,104},{48,112},{56,120},{... | collective-permute-start | bytes 3096584 | tf_op jit(solution)/shard_map/ppermute | solution.py:10
  (37 other events, 456.8 us)
Sparse Core Ops, SparseCore 0:
  13.7 36.9 all-gather.1
  413.7 76.1 reduce-scatter.1
where the time goes:
time: 507 us; the launch traced here: 500 us
  waiting for transfers between devices  229 us (45%)
  matrix products  88.6 us (17%)
  starting transfers between devices  84.7 us (17%)
  local copies, waits for them, and re-layouts  60.2 us (12%)
  other arithmetic  21.3 us (4%)
  between operations  15.6 us (3%)
    ppermute x30, waiting for transfers between devices, shifted(): return lax.ppermute(block, axis, route)  194 us
    ppermute x30, starting transfers between devices, shifted(): return lax.ppermute(block, axis, route)  82.5 us
    dot_general x16, matrix products, row_terms(): jnp.dot(match_loss_factors, gathered, preferred_element_type=jnp.float32)  38.1 us
    gather x48, local copies, waits for them, and re-layouts  31.9 us
    ppermute x2, waiting for transfers between devices, swapped(): lax.ppermute(value, axis, [(i, i ^ 1 << stride) for i in range(lax.axis_s...  27 us
    dot_general x16, matrix products, row_terms(): lax.dot_general(moving, gathered, (((1,), (1,)), ((), ())), preferred_ele...  26.9 us
    dot_general x16, matrix products, row_terms(): lax.dot_general(match_loss_factors, moving, (((0,), (0,)), ((), ())), pre...  23.6 us
    gather x3, local copies, waits for them, and re-layouts, source_owners(): return jnp.take(joined, balanced_pick(own_total, slot_count, kept_rows))  13.7 us
  transfers between devices with their start and end apart: 34, of which 27 were waited for; matrix products, arithmetic and copies ran while one was open for 27% of the time, Pallas kernels for 0%

commit v1 on v0

v1 whole, which is shorter than its diff:
```python
import jax
import jax.numpy as jnp
from jax import lax
from jax.experimental import pallas as pl
from jax.experimental.pallas import tpu as pltpu
from jax.sharding import PartitionSpec as P

EPSILON = 1e-06
R = 32
F32 = jnp.float32
BF16 = jnp.bfloat16


def normalize(rows):
    values = rows.astype(F32)
    inverse = lax.rsqrt(jnp.sum(values * values, axis=1, keepdims=True) + EPSILON)
    return values * inverse, inverse


class Copies:
    def __init__(self, send_sem, recv_sem):
        self.send_sem, self.recv_sem, self.named = send_sem, recv_sem, {}

    def send(self, name, src, dst, device):
        index = len(self.named)
        copy = pltpu.make_async_remote_copy(
            src_ref=src,
            dst_ref=dst,
            send_sem=self.send_sem.at[index],
            recv_sem=self.recv_sem.at[index],
            device_id=device,
            device_id_type=pl.DeviceIdType.MESH,
        )
        copy.start()
        self.named[name] = copy

    def wait(self, *name):
        self.named[name].wait_recv()

    def drain(self):
        for copy in self.named.values():
            copy.wait_send()


def kernel(
    img_ref, cap_ref, cnt_ref, nlm_ref, bias_ref, iout, cout,
    imgbuf, capbuf, head, tsend, trecv, wt, midx, tots, consts,
    pown, d2ds, d2dr, zsrel, zsdir, zsdep, zrrel, zrdir, zrdep, gs, gsb, ts2, tr2,
    xown, xdep, xsrel, xsdir, xsdep, xrrel, xrdir, xrdep,
    yown, ydep, ysrel, ysdir, ysdep, yrrel, yrdir, yrdep,
    send_sem, recv_sem,
):
    n_img, width = img_ref.shape
    n_slot = cap_ref.shape[0]
    kept = 9 * n_img // 2
    nk = kept // R
    nt = (n_slot - kept) // R
    cols = 4 * n_img
    rows = 8 * R
    half = n_img // 2
    blk = lax.axis_index("blk")
    grp = lax.axis_index("group")
    core, x, ylo = lax.rem(blk, 2), lax.rem(lax.div(blk, 2), 4), lax.div(blk, 8)
    z, yhi = lax.div(grp, 2), lax.rem(grp, 2)
    y = yhi * 2 + ylo

    def dev(dx=0, dy=0, dz=0):
        px, py, pz = lax.rem(x + dx + 4, 4), lax.rem(y + dy + 4, 4), lax.rem(z + dz + 4, 4)
        return ((lax.rem(py, 2) * 4 + px) * 2 + core, pz * 2 + lax.div(py, 2))

    sibling = (blk + 1 - 2 * core, grp)
    partner = (((1 - ylo) * 4 + x) * 2 + core, grp)
    copies = Copies(send_sem, recv_sem)

    barrier = pltpu.get_barrier_semaphore()
    for device in (dev(1), dev(-1), dev(0, 1), dev(0, -1), dev(0, 0, 1), dev(0, 0, -1), sibling):
        pl.semaphore_signal(barrier, inc=1, device_id=device, device_id_type=pl.DeviceIdType.MESH)
    pl.semaphore_wait(barrier, 7)

    def img_at(xr, yr, first=0, count=n_img):
        return imgbuf.at[pl.ds(xr * cols + yr * n_img + first, count)]

    def cap_at(k, core_rel, zr):
        return capbuf.at[pl.ds(k * rows + core_rel * 4 * R + zr * R, R)]

    def send_x(yr):
        copies.send(("xp", yr), img_at(0, yr), img_at(1, yr), dev(1))
        copies.send(("xm", yr), img_at(0, yr), img_at(3, yr), dev(-1))

    def relay_x(yr):
        copies.wait("xp", yr)
        copies.wait("xm", yr)
        if yr % 2 == 0:
            copies.send(("xr", yr), img_at(1, yr), img_at(2, yr), dev(1))
        else:
            copies.send(("xr", yr), img_at(3, yr), img_at(2, yr), dev(-1))

    imgbuf[pl.ds(0, n_img), :] = normalize(img_ref[...])[0].astype(BF16)
    send_x(0)

    def send_tail(t):
        tsend[t] = normalize(cap_ref[pl.ds(kept + t * R, R), :])[0].astype(BF16)
        copies.send(("t", t), tsend.at[t], trecv.at[pl.ds(t * R, R)], partner)

    send_tail(0)
    copies.send(("yp",), img_at(0, 0), img_at(0, 1), dev(0, 1))
    copies.send(("ym",), img_at(0, 0), img_at(0, 3), dev(0, -1))

    lower = (
        lax.broadcasted_iota(jnp.int32, (n_img, n_img), 0)
        >= lax.broadcasted_iota(jnp.int32, (n_img, n_img), 1)
    ).astype(F32)

    def running_ends(device, lanes):
        counts = cnt_ref[pl.ds(device[0] * 8 + device[1], 1), :].astype(F32)
        return jnp.dot((lower * counts).astype(BF16), jnp.ones((n_img, lanes), BF16), preferred_element_type=F32)

    own_ends = running_ends((blk, grp), width)
    tots[0:1, :] = own_ends[n_img - 1 :, :]
    log_row = jnp.full((1, rows), nlm_ref[0], F32)
    consts[0:1, :] = jnp.exp(log_row) * 0.5
    consts[1:2, :] = jnp.full((1, rows), bias_ref[0] * 0.5, F32)

    def before_total(first):
        position = lax.broadcasted_iota(jnp.int32, (R, width), 0) + first
        return position.astype(F32) < tots[0:1, :]

    def pack(k):
        block = normalize(cap_ref[pl.ds(k * R, R), :])[0]
        if k >= 2:
            count = (k - 1) * R
            row = (lax.broadcasted_iota(jnp.int32, (R, count), 0) + k * R).astype(F32)
            lane = lax.broadcasted_iota(jnp.int32, (R, count), 1).astype(F32)
            pick = jnp.where(row - tots[0:1, :count] == lane, 1.0, 0.0).astype(BF16)
            moved = jnp.dot(pick, trecv[pl.ds(0, count), :], preferred_element_type=F32)
            block = jnp.where(before_total(k * R), block, moved)
        capbuf[pl.ds(k * rows, R), :] = block.astype(BF16)
        copies.send(("zp", k), cap_at(k, 0, 0), cap_at(k, 0, 1), dev(0, 0, 1))
        copies.send(("zm", k), cap_at(k, 0, 0), cap_at(k, 0, 3), dev(0, 0, -1))
        copies.send(("s0", k), cap_at(k, 0, 0), cap_at(k, 1, 0), sibling)

    pack(0)
    pack(1)
    for t in range(1, nt):
        send_tail(t)

    own_part = own_ends[:, :rows]
    pair_ends = running_ends(partner, rows)
    pair_first = ((3 - 2 * ylo) * n_img).astype(F32)
    total_row = own_part[n_img - 1 :, :]
    lane = lax.broadcasted_iota(jnp.int32, (1, rows), 1)
    for k in range(nk):
        position = (lane + k * R).astype(F32)
        own_index = jnp.sum(jnp.where(own_part <= position, 1.0, 0.0), axis=0, keepdims=True)
        slot = position - total_row + float(kept)
        pair_index = jnp.sum(jnp.where(pair_ends <= slot, 1.0, 0.0), axis=0, keepdims=True)
        column = jnp.where(position < total_row, own_index, pair_first + pair_index)
        midx[k : k + 1, :] = jnp.where(lane < R, column, -1.0).astype(jnp.int32)

    def weights(k, xr, match):
        first_img = pl.multiple_of(xr * cols, cols)
        first_cap = pl.multiple_of(k * rows, rows)
        products = lax.dot_general(
            imgbuf[pl.ds(first_img, cols), :],
            capbuf[pl.ds(first_cap, rows), :],
            (((1,), (1,)), ((), ())),
            preferred_element_type=F32,
        )
        scale = consts[0:1, :]
        half_tanh = scale * jnp.tanh(products * scale + consts[1:2, :])
        if match:
            image = lax.broadcasted_iota(jnp.int32, (cols, rows), 0)
            half_tanh = half_tanh + jnp.where(image == midx[k : k + 1, :], -scale, scale)
        else:
            half_tanh = half_tanh + scale
        wt[pl.ds(first_img, cols), pl.ds(first_cap, rows)] = half_tanh.astype(BF16)

    def weights_of(xr, first, last):
        @pl.loop(first, last)
        def _(k):
            weights(k, xr, False)

    def forward(kind, k, zr):
        copies.send((kind, k), cap_at(k, 0, zr), cap_at(k, 1, zr), sibling)

    def chunk_in(k):
        for kind in ("s0", "s1", "s2", "s3"):
            copies.wait(kind, k)
        weights(k, 0, True)

    for j in range(nk):
        if j + 2 < nk:
            copies.wait("t", j)
            pack(j + 2)
        if j == 0:
            copies.wait("yp")
            copies.wait("ym")
            copies.send(("yr", 0), img_at(0, 1, 0, half), img_at(0, 2, 0, half), dev(0, 1))
            copies.send(("yr", 1), img_at(0, 3, half, half), img_at(0, 2, half, half), dev(0, -1))
            send_x(1)
            send_x(3)
        if j == 1:
            relay_x(0)
        copies.wait("zp", j)
        copies.wait("zm", j)
        if j % 2 == 0:
            copies.send(("zr", j), cap_at(j, 0, 1), cap_at(j, 0, 2), dev(0, 0, 1))
        else:
            copies.send(("zr", j), cap_at(j, 0, 3), cap_at(j, 0, 2), dev(0, 0, -1))
        forward("s1", j, 1)
        forward("s3", j, 3)
        if j == 2:
            copies.wait("yr", 0)
            copies.wait("yr", 1)
            send_x(2)
        if j >= 1:
            copies.wait("zr", j - 1)
            forward("s2", j - 1, 2)
        if j == 3:
            relay_x(1)
        if j == 5:
            relay_x(3)
        if j == 6:
            relay_x(2)
        if j >= 3:
            chunk_in(j - 3)
        if j == 7:
            weights_of(1, 0, 5)
        if j == 8:
            weights_of(3, 0, 5)
    copies.wait("zr", nk - 1)
    forward("s2", nk - 1, 2)
    for k in range(nk - 3, nk):
        chunk_in(k)
    weights_of(1, 5, nk)
    weights_of(3, 5, nk)
    for yr in (0, 1, 3, 2):
        copies.wait("xr", yr)
    weights_of(2, 0, nk)

    def caption_part(k):
        part = lax.dot_general(
            wt[:, pl.ds(k * rows, rows)], imgbuf[...], (((0,), (0,)), ((), ())), preferred_element_type=F32
        )
        pown[k] = part[: 4 * R, :]
        d2ds[k] = part[4 * R :, :].astype(BF16)
        copies.send(("d", k), d2ds.at[k], d2dr.at[k], sibling)

    def image_part(xr):
        return jnp.dot(wt[pl.ds(xr * cols, cols), :], capbuf[...], preferred_element_type=F32)

    def sign(index):
        return 1 if index % 2 == 0 else -1

    def z_first(k):
        copies.wait("d", k)
        step = sign(k)
        direct, late = (1, 3) if step == 1 else (3, 1)

        def total(zr):
            here = slice(zr * R, zr * R + R)
            return pown[k, here, :] + d2dr[k, here, :].astype(F32)

        zsrel[k] = total(2).astype(BF16)
        copies.send(("zrel", k), zsrel.at[k], zrrel.at[k], dev(0, 0, step))
        zsdir[k] = total(direct).astype(BF16)
        copies.send(("zdir", k), zsdir.at[k], zrdir.at[k], dev(0, 0, -step))
        pown[k, 0:R, :] = total(0)
        pown[k, late * R : late * R + R, :] = total(late)

    def z_late(k):
        copies.wait("zrel", k)
        step = sign(k)
        late = 3 if step == 1 else 1
        zsdep[k] = (pown[k, late * R : late * R + R, :] + zrrel[k].astype(F32)).astype(BF16)
        copies.send(("zdep", k), zsdep.at[k], zrdep.at[k], dev(0, 0, step))

    def project(first, sums, live):
        unit, inverse = normalize(cap_ref[pl.ds(first, R), :])
        grads = (sums - unit * jnp.sum(unit * sums, axis=1, keepdims=True)) * inverse
        cout[pl.ds(first, R), :] = jnp.where(live, grads, 0.0)

    def z_last(k):
        copies.wait("zdir", k)
        copies.wait("zdep", k)
        sums = pown[k, 0:R, :] + zrdir[k].astype(F32) + zrdep[k].astype(F32)
        gsb[pl.ds(k * R, R), :] = sums.astype(BF16)
        if k >= 2:
            t = k - 2
            count = kept - k * R
            row = lax.broadcasted_iota(jnp.int32, (R, count), 0).astype(F32)
            lane = (lax.broadcasted_iota(jnp.int32, (R, count), 1) + 2 * R).astype(F32)
            pick = jnp.where(row + tots[0:1, :count] == lane, 1.0, 0.0).astype(BF16)
            ts2[t] = jnp.dot(pick, gsb[pl.ds(k * R, count), :], preferred_element_type=F32).astype(BF16)
            copies.send(("tb", t), ts2.at[t], tr2.at[t], partner)
        live = before_total(k * R)
        project(k * R, jnp.where(live, sums, 0.0), live)

    def tail_last(t):
        copies.wait("tb", t)
        live = before_total(kept + t * R)
        project(kept + t * R, jnp.where(live, tr2[t].astype(F32), 0.0), live)

    def x_first(xr):
        part = image_part(xr)
        if xr == 0:
            xown[...] = part
            return
        if xr == 2:
            xsrel[...] = part.astype(BF16)
            for yr in (2, 1, 3, 0):
                here = pl.ds(yr * n_img, n_img)
                copies.send(("xrel", yr), xsrel.at[here], xrrel.at[here], dev(sign(yr)))
            return
        for yr in (2, 0, 1, 3):
            here = pl.ds(yr * n_img, n_img)
            piece = part[yr * n_img : (yr + 1) * n_img, :]
            if (sign(yr) == 1) == (xr == 3):
                xdep[here, :] = piece
            else:
                xsdir[here, :] = piece.astype(BF16)
                copies.send(("xdir", yr), xsdir.at[here], xrdir.at[here], dev(-sign(yr)))

    def x_late(yr):
        copies.wait("xrel", yr)
        here = pl.ds(yr * n_img, n_img)
        xsdep[here, :] = (xdep[here, :] + xrrel[here, :].astype(F32)).astype(BF16)
        copies.send(("xdep", yr), xsdep.at[here], xrdep.at[here], dev(sign(yr)))

    low, high = pl.ds(0, half), pl.ds(half, half)

    def x_last(yr):
        copies.wait("xdir", yr)
        copies.wait("xdep", yr)
        here = pl.ds(yr * n_img, n_img)
        sums = xown[here, :] + xrdir[here, :].astype(F32) + xrdep[here, :].astype(F32)
        if yr == 0:
            yown[...] = sums
        elif yr == 2:
            ysrel[...] = sums.astype(BF16)
            copies.send(("yrel", 0), ysrel.at[low], yrrel.at[low], dev(0, 1))
            copies.send(("yrel", 1), ysrel.at[high], yrrel.at[high], dev(0, -1))
        elif yr == 1:
            ysdir[low, :] = sums[:half, :].astype(BF16)
            copies.send(("ydir", 0), ysdir.at[low], yrdir.at[low], dev(0, -1))
            ydep[high, :] = sums[half:, :]
        else:
            ysdir[high, :] = sums[half:, :].astype(BF16)
            copies.send(("ydir", 1), ysdir.at[high], yrdir.at[high], dev(0, 1))
            ydep[low, :] = sums[:half, :]

    def y_late(part):
        copies.wait("yrel", part)
        here = (low, high)[part]
        ysdep[here, :] = (ydep[here, :] + yrrel[here, :].astype(F32)).astype(BF16)
        copies.send(("ydep", part), ysdep.at[here], yrdep.at[here], dev(0, (1, -1)[part]))

    caption_part(8)
    x_first(2)
    z_first(8)
    caption_part(7)
    x_first(1)
    z_first(7)
    caption_part(6)
    x_first(3)
    z_first(6)
    caption_part(5)
    z_late(8)
    x_first(0)
    z_first(5)
    caption_part(4)
    z_late(7)
    for k in (3, 2, 1, 0):
        z_first(k + 1)
        caption_part(k)
        z_late(k + 3)
    z_first(0)
    x_late(2)
    z_last(8)
    z_late(2)
    x_late(1)
    z_last(7)
    x_late(3)
    z_late(1)
    z_last(6)
    x_late(0)
    z_late(0)
    z_last(5)
    z_last(4)
    x_last(2)
    z_last(3)
    x_last(1)
    x_last(3)
    y_late(0)
    y_late(1)
    z_last(2)
    x_last(0)
    z_last(1)
    z_last(0)
    for t in reversed(range(nt)):
        tail_last(t)
    for name in (("ydir", 0), ("ydir", 1), ("ydep", 0), ("ydep", 1)):
        copies.wait(*name)
    sums = yown[...] + yrdir[...].astype(F32) + yrdep[...].astype(F32)
    unit, inverse = normalize(img_ref[...])
    iout[...] = (sums - unit * jnp.sum(unit * sums, axis=1, keepdims=True)) * inverse
    copies.drain()


def shards(image_embed, caption_vectors, caption_counts, natural_log_multiplier, match_odds_offset):
    n_img, width = image_embed.shape
    n_slot = caption_vectors.shape[0]
    kept = 9 * n_img // 2
    nk, nt = kept // R, (n_slot - kept) // R
    cols, rows = 4 * n_img, 8 * R
    vmem = pl.BlockSpec(memory_space=pltpu.VMEM)
    smem = pl.BlockSpec(memory_space=pltpu.SMEM)

    def buf(*shape, dtype=BF16):
        return pltpu.VMEM((*shape, width), dtype)

    scratch = [
        buf(4 * cols),
        buf(nk * rows),
        buf(R),
        buf(nt, R),
        buf(nt * R),
        pltpu.VMEM((4 * cols, nk * rows), BF16),
        pltpu.VMEM((16, rows), jnp.int32),
        pltpu.VMEM((8, width), F32),
        pltpu.VMEM((8, rows), F32),
        buf(nk, 4 * R, dtype=F32),
        buf(nk, 4 * R),
        buf(nk, 4 * R),
        *[buf(nk, R)] * 6,
        buf(R, dtype=F32),
        buf(kept),
        buf(nt, R),
        buf(nt, R),
        *[buf(cols, dtype=F32)] * 2,
        *[buf(cols)] * 6,
        *[buf(n_img, dtype=F32)] * 2,
        *[buf(n_img)] * 6,
        pltpu.SemaphoreType.DMA((160,)),
        pltpu.SemaphoreType.DMA((160,)),
    ]
    return pl.pallas_call(
        kernel,
        out_shape=(
            jax.ShapeDtypeStruct((n_img, width), F32),
            jax.ShapeDtypeStruct((n_slot, width), F32),
        ),
        in_specs=[vmem, vmem, vmem, smem, smem],
        out_specs=(vmem, vmem),
        scratch_shapes=scratch,
        compiler_params=pltpu.CompilerParams(
            collective_id=0, has_side_effects=True, vmem_limit_bytes=60 * 1024 * 1024
        ),
    )(image_embed, caption_vectors, caption_counts.reshape(-1, n_img), natural_log_multiplier, match_odds_offset)


def solution(mesh):
    placed = (P(("blk", "group"), None), P(("blk", "group"), None), P(), P(), P())
    return jax.shard_map(
        shards,
        mesh=mesh,
        in_specs=placed,
        out_specs=(P(("blk", "group"), None), P(("blk", "group"), None)),
        check_vma=False,
    )
```

time: 507 us -> 104 us (0.21); the launches traced: 500 us -> 104 us
  waiting for transfers between devices: 229 us -> 0 us
  Pallas kernels: 0 us -> 95.6 us
  matrix products: 88.6 us -> 0 us
  starting transfers between devices: 84.7 us -> 0 us
  local copies, waits for them, and re-layouts: 60.2 us -> 6.38 us
  other arithmetic: 21.3 us -> 0 us
  between operations: 15.6 us -> 1.93 us
    ppermute x32 -> x0, waiting for transfers between devices: 221 us -> none  [the longest x30 194 us: shifted(): return lax.ppermute(block, axis, route)]
    pallas_call x0 -> x1, Pallas kernels: none -> 95.6 us  [shards(): pl.pallas_call(kernel, out_shape=(jax.ShapeDtypeStruct((n_img, width), F3...]
    dot_general x48 -> x0, matrix products: 88.6 us -> none  [the longest x16 38.1 us: row_terms(): jnp.dot(match_loss_factors, gathered, preferred_element_type=jnp.float32)]
    ppermute x32 -> x0, starting transfers between devices: 84.7 us -> none  [the longest x30 82.5 us: shifted(): return lax.ppermute(block, axis, route)]
    gather x53 -> x0, local copies, waits for them, and re-layouts: 48.9 us -> none
    reduce_scatter x1 -> x0, waiting for transfers between devices: 7.45 us -> none  [shards(): lax.psum_scatter(image_acc, 'blk', scatter_dimension=0, tiled=True)]
    select_n x11 -> x0, other arithmetic: 5.63 us -> none  [the longest x1 1.95 us: shards(): jnp.where((home_owner >= 0)[:, None], (slot_grads - caption_unit * jnp.su...]
    while x56 -> x0, local copies, waits for them, and re-layouts: 5.4 us -> none
  transfers between devices with their start and end apart: 34 -> 0, of which waited for: 27 -> 0; matrix products, arithmetic and copies ran while one was open for 27% -> 0% of each run, Pallas kernels for 0% -> 0%
where the time goes in v1:
time: 104 us
  Pallas kernels  95.6 us (92%)
  local copies, waits for them, and re-layouts  6.38 us (6%)
  between operations  1.93 us (2%)
    pallas_call x1, Pallas kernels, shards(): pl.pallas_call(kernel, out_shape=(jax.ShapeDtypeStruct((n_img, width), F3...  95.6 us
    unnamed x2, local copies, waits for them, and re-layouts  4.92 us

profile of v1, /device:TPU:1, one launch (start us, length us, event | category | flops | bytes accessed | tf_op | source)
XLA Modules:
  0.0 104.0 jit_solution(12463207403844572456)
XLA Ops:
  1.9 1.5 %reshape.7.cnt_ref = s32[128,64]{1,0:T(8,128)} reshape(s32[8192]{0:T(1024)} %param.7) | data formatting | bytes 65536 | tf_op jit(solution)/shard_map/reshape | solution.py:459
  3.4 95.6 %shard_map.68 = (f32[64,1152]{1,0:T(8,128)}, f32[512,1152]{1,0:T(8,128)}) custom-call(bf16[64,1152]{1,0:T(8,128)(2,1)} %img_ref.1, bf16[512,1152]{1,0:T(8,128)(2,1)} %cap_ref.1, s32[128,64]{1,0:T(8,128)} %reshape.7.cnt_ref, f32[1]{0:T(128)S(6)} %copy.9.nlm_ref, f32[1]{0:T(128)S(6)} %copy.10.bias_ref), custom_call_target="tpu_custom_call" | custom-call | tf_op jit(solution)/shard_map/pallas_call | solution.py:447
  99.0 1.7 %copy.11 = f32[64,1152]{1,0:T(8,128)} copy(f32[64,1152]{1,0:T(8,128)} %get-tuple-element.4) | data formatting | bytes 589824
  100.7 3.2 %copy.12 = f32[512,1152]{1,0:T(8,128)} copy(f32[512,1152]{1,0:T(8,128)} %get-tuple-element.5) | data formatting | bytes 4718592

commit v2 on v1

v2 whole, which is shorter than its diff:
```python
import jax
import jax.numpy as jnp
from jax import lax
from jax.experimental import pallas as pl
from jax.experimental.pallas import tpu as pltpu
from jax.sharding import PartitionSpec as P

EPSILON = 1e-06
R = 32
F32 = jnp.float32
BF16 = jnp.bfloat16


YPOS = 2
ORDER = (
    ("sx", 0), ("t", 0), ("t", 1), ("p", 0), ("p", 1), ("t", 2), ("t", 3), ("t", 4), ("t", 5), ("t", 6), ("p", 2),
    ("f", 0, 1), ("f", 0, 3), ("rx", 0), ("p", 3), ("ry", 3), ("sx", 3), ("f", 1, 3), ("f", 1, 1), ("f", 2, 1),
    ("f", 2, 3), ("ry", 1), ("sx", 1), ("f", 3, 3), ("f", 0, 2), ("p", 4), ("f", 1, 2), ("f", 3, 1), ("rx", 3),
    ("p", 5), ("f", 2, 2), ("f", 3, 2), ("p", 6), ("f", 4, 1), ("rx", 1), ("f", 4, 3), ("p", 7), ("f", 5, 1),
    ("f", 5, 3), ("p", 8), ("f", 6, 1), ("f", 6, 3), ("sx", 2), ("A", 0, 0), ("A", 1, 0), ("A", 2, 0), ("A", 3, 0),
    ("f", 4, 2), ("f", 7, 3), ("A", 4, 0), ("f", 7, 1), ("f", 5, 2), ("f", 8, 1), ("A", 5, 0), ("f", 8, 3), ("rx", 2),
    ("A", 5, 1), ("A", 1, 1), ("A", 2, 3), ("A", 2, 1), ("A", 4, 3), ("A", 0, 3), ("A", 3, 1), ("A", 3, 3),
    ("A", 1, 3), ("A", 5, 3), ("f", 6, 2), ("A", 0, 1), ("A", 4, 1), ("f", 7, 2), ("f", 8, 2), ("A", 6, 0),
    ("A", 6, 1), ("A", 6, 3), ("A", 7, 3), ("A", 8, 3), ("A", 7, 1), ("A", 8, 1), ("A", 7, 0), ("A", 8, 0),
    ("C", 1, 0), ("A", 8, 2), ("B", 8), ("A", 6, 2), ("A", 4, 2), ("A", 1, 2), ("A", 2, 2), ("A", 0, 2), ("A", 7, 2),
    ("B", 7), ("A", 3, 2), ("A", 5, 2), ("zf", 8), ("B", 6), ("C", 2, 0), ("zf", 7), ("B", 5), ("C", 0, 1), ("zf", 6),
    ("C", 2, 1), ("zl", 8), ("C", 0, 0), ("zf", 5), ("B", 4), ("zl", 7), ("B", 3), ("C", 3, 0), ("xl", 2), ("zl", 6),
    ("C", 3, 1), ("zf", 4), ("zz", 8), ("zf", 3), ("zl", 5), ("B", 2), ("B", 1), ("zz", 7), ("xl", 0), ("C", 1, 1),
    ("xl", 1), ("zz", 6), ("zf", 2), ("B", 0), ("e", 6), ("xl", 3), ("xz", 2), ("zl", 4), ("zl", 3), ("zf", 1),
    ("e", 5), ("zf", 0), ("zz", 5), ("e", 4), ("zl", 2), ("xz", 1), ("yz", 1), ("zz", 4), ("zz", 3), ("e", 3),
    ("xz", 3), ("zl", 1), ("yz", 0), ("zl", 0), ("xz", 0), ("zz", 2), ("e", 2), ("zz", 1), ("zz", 0), ("end",),
    ("e", 1), ("e", 0),
)


def normalize(rows):
    values = rows.astype(F32)
    inverse = lax.rsqrt(jnp.sum(values * values, axis=1, keepdims=True) + EPSILON)
    return values * inverse, inverse


class Copies:
    def __init__(self, send_sem, recv_sem):
        self.send_sem, self.recv_sem, self.named, self.open = send_sem, recv_sem, {}, set()

    def send(self, name, src, dst, device):
        index = len(self.named)
        copy = pltpu.make_async_remote_copy(
            src_ref=src,
            dst_ref=dst,
            send_sem=self.send_sem.at[index],
            recv_sem=self.recv_sem.at[index],
            device_id=device,
            device_id_type=pl.DeviceIdType.MESH,
        )
        copy.start()
        self.named[name] = copy
        self.open.add(name)

    def wait(self, *name):
        if name in self.open:
            self.named[name].wait_recv()
            self.open.remove(name)

    def drain(self):
        for name, copy in self.named.items():
            self.wait(*name)
            copy.wait_send()


def kernel(
    img_ref, cap_ref, cnt_ref, nlm_ref, bias_ref, iout, cout,
    imgbuf, capbuf, head, tsend, trecv, wt, midx, tots, consts,
    pown, d2ds, d2dr, zsrel, zsdir, zsdep, zrrel, zrdir, zrdep, gs, gsb, ts2, tr2,
    xown, xdep, xsrel, xsdir, xsdep, xrrel, xrdir, xrdep,
    yown, ydep, ysrel, ysdir, ysdep, yrrel, yrdir, yrdep,
    send_sem, recv_sem,
):
    n_img, width = img_ref.shape
    n_slot = cap_ref.shape[0]
    kept = 9 * n_img // 2
    nk = kept // R
    nt = (n_slot - kept) // R
    cols = 4 * n_img
    rows = 8 * R
    half = n_img // 2
    blk = lax.axis_index("blk")
    grp = lax.axis_index("group")
    core, x, ylo = lax.rem(blk, 2), lax.rem(lax.div(blk, 2), 4), lax.div(blk, 8)
    z, yhi = lax.div(grp, 2), lax.rem(grp, 2)
    y = yhi * 2 + ylo
    near = 1 - 2 * ylo

    def dev(dx=0, dy=0, dz=0):
        px, py, pz = lax.rem(x + dx + 4, 4), lax.rem(y + dy + 4, 4), lax.rem(z + dz + 4, 4)
        return ((lax.rem(py, 2) * 4 + px) * 2 + core, pz * 2 + lax.div(py, 2))

    sibling = (blk + 1 - 2 * core, grp)
    partner = (((1 - ylo) * 4 + x) * 2 + core, grp)
    copies = Copies(send_sem, recv_sem)

    barrier = pltpu.get_barrier_semaphore()
    for device in (dev(1), dev(-1), dev(0, 1), dev(0, -1), dev(0, 0, 1), dev(0, 0, -1), sibling):
        pl.semaphore_signal(barrier, inc=1, device_id=device, device_id_type=pl.DeviceIdType.MESH)

    place = (0, 2, 1, 3)

    def img_at(xr, yr, first=0, count=n_img):
        return imgbuf.at[pl.ds(xr * cols + place[yr] * n_img + first, count)]

    def cap_at(k, core_rel, zr):
        return capbuf.at[pl.ds(k * rows + core_rel * 4 * R + zr * R, R)]

    def sign(index):
        return 1 if index % 2 == 0 else -1

    imgbuf[pl.ds(0, n_img), :] = normalize(img_ref[...])[0].astype(BF16)
    for t in range(nt):
        tsend[t] = normalize(cap_ref[pl.ds(kept + t * R, R), :])[0].astype(BF16)

    two = 2 * n_img
    image_row = lax.broadcasted_iota(jnp.int32, (n_img, two), 0)
    image_lane = lax.broadcasted_iota(jnp.int32, (n_img, two), 1)

    def running_ends(device, lanes):
        number = device[0] * 8 + device[1]
        counts = cnt_ref[pl.ds(lax.div(number, 2), 1), :].astype(F32)
        local = image_lane - lax.rem(number, 2) * n_img
        lower = jnp.where(jnp.logical_and(local >= 0, local <= image_row), counts, 0.0)
        return jnp.dot(lower.astype(BF16), jnp.ones((two, lanes), BF16), preferred_element_type=F32)

    own_ends = running_ends((blk, grp), width)
    tots[0:1, :] = own_ends[n_img - 1 :, :]
    log_row = jnp.full((1, rows), nlm_ref[0], F32)
    consts[0:1, :] = jnp.exp(log_row) * 0.5
    consts[1:2, :] = jnp.full((1, rows), bias_ref[0] * 0.5, F32)

    own_part = own_ends[:, :rows]
    pair_ends = running_ends(partner, rows)
    total_row = own_part[n_img - 1 :, :]
    lane = lax.broadcasted_iota(jnp.int32, (1, rows), 1)
    for k in range(nk):
        position = (lane + k * R).astype(F32)
        own_index = jnp.sum(jnp.where(own_part <= position, 1.0, 0.0), axis=0, keepdims=True)
        slot = position - total_row + float(kept)
        pair_index = jnp.sum(jnp.where(pair_ends <= slot, 1.0, 0.0), axis=0, keepdims=True)
        column = jnp.where(position < total_row, own_index, float(place[1] * n_img) + pair_index)
        midx[k : k + 1, :] = jnp.where(lane < R, column, -1.0).astype(jnp.int32)

    pl.semaphore_wait(barrier, 7)

    def before_total(first):
        position = lax.broadcasted_iota(jnp.int32, (R, width), 0) + first
        return position.astype(F32) < tots[0:1, :]

    def send_x(yr):
        if yr == 2:
            copies.wait("y2", 1)
            copies.wait("y2", 3)
        elif yr:
            copies.wait("y", yr)
        copies.send(("xp", yr), img_at(0, yr), img_at(1, yr), dev(1))
        copies.send(("xm", yr), img_at(0, yr), img_at(3, yr), dev(-1))

    def relay_x(yr):
        kind, xr = ("xp", 1) if yr % 2 == 0 else ("xm", 3)
        copies.wait(kind, yr)
        copies.send(("xr", yr), img_at(xr, yr), img_at(2, yr), dev(sign(yr)))

    def relay_y(yr):
        copies.wait("y", yr)
        first, step = (0, -near) if yr == 1 else (half, near)
        copies.send(("y2", yr), img_at(0, yr, first, half), img_at(0, 2, first, half), dev(0, step))

    def tail(t):
        copies.send(("t", t), tsend.at[t], trecv.at[pl.ds(t * R, R)], partner)
        if t == YPOS - 1:
            copies.send(("y", 1), img_at(0, 0), img_at(0, 1), partner)
            copies.send(("y", 3), img_at(0, 0), img_at(0, 3), dev(0, -near))

    def pack(k):
        block = normalize(cap_ref[pl.ds(k * R, R), :])[0]
        if k >= 2:
            copies.wait("t", k - 2)
            count = (k - 1) * R
            row = (lax.broadcasted_iota(jnp.int32, (R, count), 0) + k * R).astype(F32)
            lane = lax.broadcasted_iota(jnp.int32, (R, count), 1).astype(F32)
            pick = jnp.where(row - tots[0:1, :count] == lane, 1.0, 0.0).astype(BF16)
            moved = jnp.dot(pick, trecv[pl.ds(0, count), :], preferred_element_type=F32)
            block = jnp.where(before_total(k * R), block, moved)
        capbuf[pl.ds(k * rows, R), :] = block.astype(BF16)
        copies.send(("zp", k), cap_at(k, 0, 0), cap_at(k, 0, 1), dev(0, 0, 1))
        copies.send(("zm", k), cap_at(k, 0, 0), cap_at(k, 0, 3), dev(0, 0, -1))
        copies.send(("s", 0, k), cap_at(k, 0, 0), cap_at(k, 1, 0), sibling)

    def forward(k, zr):
        copies.wait(("", "zp", "zr", "zm")[zr], k)
        if zr != 2 and (zr == 1) == (k % 2 == 0):
            copies.send(("zr", k), cap_at(k, 0, zr), cap_at(k, 0, 2), dev(0, 0, sign(k)))
        copies.send(("s", zr, k), cap_at(k, 0, zr), cap_at(k, 1, zr), sibling)

    def weights(k, xr):
        for zr in range(4):
            copies.wait("s", zr, k)
        if xr == 0:
            for name in (("y", 1), ("y", 3), ("y2", 1), ("y2", 3)):
                copies.wait(*name)
        else:
            for yr in range(4):
                copies.wait(("", "xp", "xr", "xm")[xr], yr)
        products = lax.dot_general(
            imgbuf[pl.ds(xr * cols, cols), :],
            capbuf[pl.ds(k * rows, rows), :],
            (((1,), (1,)), ((), ())),
            preferred_element_type=F32,
        )
        scale = consts[0:1, :]
        half_tanh = scale * jnp.tanh(products * scale + consts[1:2, :])
        if xr == 0:
            image = lax.broadcasted_iota(jnp.int32, (cols, rows), 0)
            half_tanh = half_tanh + jnp.where(image == midx[k : k + 1, :], -scale, scale)
        else:
            half_tanh = half_tanh + scale
        wt[pl.ds(xr * cols, cols), pl.ds(k * rows, rows)] = half_tanh.astype(BF16)

    def caption_part(k):
        part = lax.dot_general(
            wt[:, pl.ds(k * rows, rows)], imgbuf[...], (((0,), (0,)), ((), ())), preferred_element_type=F32
        )
        pown[k] = part[: 4 * R, :]
        d2ds[k] = part[4 * R :, :].astype(BF16)
        copies.send(("d", k), d2ds.at[k], d2dr.at[k], sibling)

    def z_first(k):
        copies.wait("d", k)
        step = sign(k)
        direct, late = (1, 3) if step == 1 else (3, 1)

        def total(zr):
            here = slice(zr * R, zr * R + R)
            return pown[k, here, :] + d2dr[k, here, :].astype(F32)

        zsrel[k] = total(2).astype(BF16)
        copies.send(("zrel", k), zsrel.at[k], zrrel.at[k], dev(0, 0, step))
        zsdir[k] = total(direct).astype(BF16)
        copies.send(("zdir", k), zsdir.at[k], zrdir.at[k], dev(0, 0, -step))
        pown[k, 0:R, :] = total(0)
        pown[k, late * R : late * R + R, :] = total(late)

    def z_late(k):
        copies.wait("zrel", k)
        step = sign(k)
        late = 3 if step == 1 else 1
        zsdep[k] = (pown[k, late * R : late * R + R, :] + zrrel[k].astype(F32)).astype(BF16)
        copies.send(("zdep", k), zsdep.at[k], zrdep.at[k], dev(0, 0, step))

    def project(first, sums, live):
        unit, inverse = normalize(cap_ref[pl.ds(first, R), :])
        grads = (sums - unit * jnp.sum(unit * sums, axis=1, keepdims=True)) * inverse
        cout[pl.ds(first, R), :] = jnp.where(live, grads, 0.0)

    def z_last(k):
        copies.wait("zdir", k)
        copies.wait("zdep", k)
        sums = pown[k, 0:R, :] + zrdir[k].astype(F32) + zrdep[k].astype(F32)
        gsb[pl.ds(k * R, R), :] = sums.astype(BF16)
        if k >= 2:
            t = k - 2
            count = kept - k * R
            row = lax.broadcasted_iota(jnp.int32, (R, count), 0).astype(F32)
            lane = (lax.broadcasted_iota(jnp.int32, (R, count), 1) + 2 * R).astype(F32)
            pick = jnp.where(row + tots[0:1, :count] == lane, 1.0, 0.0).astype(BF16)
            ts2[t] = jnp.dot(pick, gsb[pl.ds(k * R, count), :], preferred_element_type=F32).astype(BF16)
            copies.send(("tb", t), ts2.at[t], tr2.at[t], partner)
        live = before_total(k * R)
        project(k * R, jnp.where(live, sums, 0.0), live)

    def tail_last(t):
        copies.wait("tb", t)
        live = before_total(kept + t * R)
        project(kept + t * R, jnp.where(live, tr2[t].astype(F32), 0.0), live)

    def image_part(xr, h):
        first = xr * cols + h * two
        part = jnp.dot(wt[pl.ds(first, two), :], capbuf[...], preferred_element_type=F32)
        here = pl.ds(h * two, two)
        pairs = [(yr, pl.ds(place[yr] * n_img, n_img)) for yr in ((2, 0) if h == 0 else (1, 3))]
        if xr == 0:
            xown[here, :] = part
        elif xr == 2:
            xsrel[here, :] = part.astype(BF16)
            for yr, at in pairs:
                copies.send(("xrel", yr), xsrel.at[at], xrrel.at[at], dev(sign(yr)))
        elif (h == 0) == (xr == 3):
            xdep[here, :] = part
        else:
            xsdir[here, :] = part.astype(BF16)
            for yr, at in pairs:
                copies.send(("xdir", yr), xsdir.at[at], xrdir.at[at], dev(-sign(yr)))

    def x_late(yr):
        copies.wait("xrel", yr)
        here = pl.ds(place[yr] * n_img, n_img)
        xsdep[here, :] = (xdep[here, :] + xrrel[here, :].astype(F32)).astype(BF16)
        copies.send(("xdep", yr), xsdep.at[here], xrdep.at[here], dev(sign(yr)))

    low, high = pl.ds(0, half), pl.ds(half, half)

    def x_last(yr):
        copies.wait("xdir", yr)
        copies.wait("xdep", yr)
        here = pl.ds(place[yr] * n_img, n_img)
        sums = xown[here, :] + xrdir[here, :].astype(F32) + xrdep[here, :].astype(F32)
        if yr == 0:
            yown[...] = sums
        elif yr == 2:
            ysrel[...] = sums.astype(BF16)
            copies.send(("yrel", 0), ysrel.at[low], yrrel.at[low], partner)
            copies.send(("yrel", 1), ysrel.at[high], yrrel.at[high], dev(0, -near))
        elif yr == 1:
            ysdir[low, :] = sums[:half, :].astype(BF16)
            copies.send(("ydir", 1), ysdir.at[low], yrdir.at[low], partner)
            ydep[high, :] = sums[half:, :]
        else:
            ysdir[high, :] = sums[half:, :].astype(BF16)
            copies.send(("ydir", 3), ysdir.at[high], yrdir.at[high], dev(0, -near))
            ydep[low, :] = sums[:half, :]

    def y_late(part):
        copies.wait("yrel", part)
        here = (low, high)[part]
        ysdep[here, :] = (ydep[here, :] + yrrel[here, :].astype(F32)).astype(BF16)
        copies.send(("ydep", part), ysdep.at[here], yrdep.at[here], partner if part else dev(0, -near))

    def finish():
        for name in (("ydir", 1), ("ydir", 3), ("ydep", 0), ("ydep", 1)):
            copies.wait(*name)
        sums = yown[...] + yrdir[...].astype(F32) + yrdep[...].astype(F32)
        unit, inverse = normalize(img_ref[...])
        iout[...] = (sums - unit * jnp.sum(unit * sums, axis=1, keepdims=True)) * inverse

    actions = dict(
        sx=send_x, rx=relay_x, ry=relay_y, t=tail, p=pack, f=forward, A=weights, B=caption_part, C=image_part,
        zf=z_first, zl=z_late, zz=z_last, e=tail_last, xl=x_late, xz=x_last, yz=y_late, end=finish,
    )
    for kind, *numbers in ORDER:
        actions[kind](*numbers)
    copies.drain()


def shards(image_embed, caption_vectors, caption_counts, natural_log_multiplier, match_odds_offset):
    n_img, width = image_embed.shape
    n_slot = caption_vectors.shape[0]
    kept = 9 * n_img // 2
    nk, nt = kept // R, (n_slot - kept) // R
    cols, rows = 4 * n_img, 8 * R
    vmem = pl.BlockSpec(memory_space=pltpu.VMEM)
    smem = pl.BlockSpec(memory_space=pltpu.SMEM)

    def buf(*shape, dtype=BF16):
        return pltpu.VMEM((*shape, width), dtype)

    scratch = [
        buf(4 * cols),
        buf(nk * rows),
        buf(R),
        buf(nt, R),
        buf(nt * R),
        pltpu.VMEM((4 * cols, nk * rows), BF16),
        pltpu.VMEM((16, rows), jnp.int32),
        pltpu.VMEM((8, width), F32),
        pltpu.VMEM((8, rows), F32),
        buf(nk, 4 * R, dtype=F32),
        buf(nk, 4 * R),
        buf(nk, 4 * R),
        *[buf(nk, R)] * 6,
        buf(R, dtype=F32),
        buf(kept),
        buf(nt, R),
        buf(nt, R),
        *[buf(cols, dtype=F32)] * 2,
        *[buf(cols)] * 6,
        *[buf(n_img, dtype=F32)] * 2,
        *[buf(n_img)] * 6,
        pltpu.SemaphoreType.DMA((160,)),
        pltpu.SemaphoreType.DMA((160,)),
    ]
    return pl.pallas_call(
        kernel,
        out_shape=(
            jax.ShapeDtypeStruct((n_img, width), F32),
            jax.ShapeDtypeStruct((n_slot, width), F32),
        ),
        in_specs=[vmem, vmem, vmem, smem, smem],
        out_specs=(vmem, vmem),
        scratch_shapes=scratch,
        compiler_params=pltpu.CompilerParams(
            collective_id=0, has_side_effects=True, vmem_limit_bytes=60 * 1024 * 1024
        ),
    )(image_embed, caption_vectors, caption_counts.reshape(-1, 2 * n_img), natural_log_multiplier, match_odds_offset)


def solution(mesh):
    placed = (P(("blk", "group"), None), P(("blk", "group"), None), P(), P(), P())
    return jax.shard_map(
        shards,
        mesh=mesh,
        in_specs=placed,
        out_specs=(P(("blk", "group"), None), P(("blk", "group"), None)),
        check_vma=False,
    )
```

time: 104 us -> 82.8 us (0.80)
  Pallas kernels: 95.6 us -> 75.8 us
  local copies, waits for them, and re-layouts: 6.38 us -> 4.92 us
    pallas_call x1, Pallas kernels: 95.6 us -> 75.8 us  [shards(): pl.pallas_call(kernel, out_shape=(jax.ShapeDtypeStruct((n_img, width), F3...]
    reshape x1 -> x0, local copies, waits for them, and re-layouts: 1.46 us -> none  [shards(): caption_counts.reshape(-1, n_img)]
where the time goes in v2:
time: 82.8 us; the launch traced here: 82.6 us
  Pallas kernels  75.8 us (92%)
  local copies, waits for them, and re-layouts  4.92 us (6%)
  between operations  1.93 us (2%)
    pallas_call x1, Pallas kernels, shards(): pl.pallas_call(kernel, out_shape=(jax.ShapeDtypeStruct((n_img, width), F3...  75.8 us
    unnamed x2, local copies, waits for them, and re-layouts  4.92 us

profile of v2, /device:TPU:1, one launch (start us, length us, event | category | flops | bytes accessed | tf_op | source)
XLA Modules:
  0.0 82.6 jit_solution(3891802876549385263)
XLA Ops:
  1.9 75.8 %shard_map.68 = (f32[64,1152]{1,0:T(8,128)}, f32[512,1152]{1,0:T(8,128)}) custom-call(bf16[64,1152]{1,0:T(8,128)(2,1)} %img_ref.1, bf16[512,1152]{1,0:T(8,128)(2,1)} %cap_ref.1, s32[64,128]{1,0:T(8,128)} %bitcast.1, f32[1]{0:T(128)S(6)} %copy.9.nlm_ref, f32[1]{0:T(128)S(6)} %copy.10.bias_ref), custom_call_target="tpu_custom_call" | custom-call | tf_op jit(solution)/shard_map/pallas_call | solution.py:388
  77.7 1.7 %copy.11 = f32[64,1152]{1,0:T(8,128)} copy(f32[64,1152]{1,0:T(8,128)} %get-tuple-element.4) | data formatting | bytes 589824
  79.4 3.2 %copy.12 = f32[512,1152]{1,0:T(8,128)} copy(f32[512,1152]{1,0:T(8,128)} %get-tuple-element.5) | data formatting | bytes 4718592

commit v3 on v2

--- a/solution.py
+++ b/solution.py
@@ -69,13 +69,19 @@
 
 
 def kernel(
-    img_ref, cap_ref, cnt_ref, nlm_ref, bias_ref, iout, cout,
-    imgbuf, capbuf, head, tsend, trecv, wt, midx, tots, consts,
+    img_hbm, cap_hbm, cnt_hbm, nlm_ref, bias_ref, iout, cout,
+    img_ref, cap_ref, cnt_ref, load_sem, imgbuf, capbuf, head, tsend, trecv, wt, midx, tots, consts,
     pown, d2ds, d2dr, zsrel, zsdir, zsdep, zrrel, zrdir, zrdep, gs, gsb, ts2, tr2,
     xown, xdep, xsrel, xsdir, xsdep, xrrel, xrdir, xrdep,
     yown, ydep, ysrel, ysdir, ysdep, yrrel, yrdir, yrdep,
     send_sem, recv_sem,
 ):
+    loads = [
+        pltpu.make_async_copy(src, dst, load_sem.at[i])
+        for i, (src, dst) in enumerate(((img_hbm, img_ref), (cap_hbm, cap_ref), (cnt_hbm, cnt_ref)))
+    ]
+    for load in loads:
+        load.start()
     n_img, width = img_ref.shape
     n_slot = cap_ref.shape[0]
     kept = 9 * n_img // 2
@@ -114,10 +120,13 @@
     def sign(index):
         return 1 if index % 2 == 0 else -1
 
+    loads[0].wait()
     imgbuf[pl.ds(0, n_img), :] = normalize(img_ref[...])[0].astype(BF16)
+    loads[1].wait()
     for t in range(nt):
         tsend[t] = normalize(cap_ref[pl.ds(kept + t * R, R), :])[0].astype(BF16)
 
+    loads[2].wait()
     two = 2 * n_img
     image_row = lax.broadcasted_iota(jnp.int32, (n_img, two), 0)
     image_lane = lax.broadcasted_iota(jnp.int32, (n_img, two), 1)
@@ -356,11 +365,16 @@
     cols, rows = 4 * n_img, 8 * R
     vmem = pl.BlockSpec(memory_space=pltpu.VMEM)
     smem = pl.BlockSpec(memory_space=pltpu.SMEM)
+    anywhere = pl.BlockSpec(memory_space=pl.ANY)
 
     def buf(*shape, dtype=BF16):
         return pltpu.VMEM((*shape, width), dtype)
 
     scratch = [
+        buf(n_img),
+        buf(n_slot),
+        pltpu.VMEM((caption_counts.shape[0] // (2 * n_img), 2 * n_img), jnp.int32),
+        pltpu.SemaphoreType.DMA((3,)),
         buf(4 * cols),
         buf(nk * rows),
         buf(R),
@@ -388,10 +402,10 @@
     return pl.pallas_call(
         kernel,
         out_shape=(
-            jax.ShapeDtypeStruct((n_img, width), F32),
-            jax.ShapeDtypeStruct((n_slot, width), F32),
+            pltpu.VMEM((n_img, width), F32),
+            pltpu.VMEM((n_slot, width), F32),
         ),
-        in_specs=[vmem, vmem, vmem, smem, smem],
+        in_specs=[anywhere, anywhere, anywhere, smem, smem],
         out_specs=(vmem, vmem),
         scratch_shapes=scratch,
         compiler_params=pltpu.CompilerParams(

time: 82.8 us -> 77.3 us (0.934)
  local copies, waits for them, and re-layouts: 4.92 us -> 2.12 us
  Pallas kernels: 75.8 us -> 73.1 us
    unnamed x2, local copies, waits for them, and re-layouts: 4.92 us -> 2.12 us
    pallas_call x1, Pallas kernels: 75.8 us -> 73.1 us  [shards(): pl.pallas_call(kernel, out_shape=(pltpu.VMEM((n_img, width), F32), pltpu....]
where the time goes in v3:
time: 77.3 us; the launch traced here: 77.1 us
  Pallas kernels  73.1 us (95%)
  local copies, waits for them, and re-layouts  2.12 us (3%)
  between operations  1.93 us (2%)
    pallas_call x1, Pallas kernels, shards(): pl.pallas_call(kernel, out_shape=(pltpu.VMEM((n_img, width), F32), pltpu....  73.1 us
    unnamed x2, local copies, waits for them, and re-layouts  2.12 us

profile of v3, /device:TPU:1, one launch (start us, length us, event | category | flops | bytes accessed | tf_op | source)
XLA Modules:
  0.0 77.1 jit_solution(7052806806639041968)
XLA Ops:
  1.9 73.1 %shard_map.68 = (f32[64,1152]{1,0:T(8,128)S(1)}, f32[512,1152]{1,0:T(8,128)S(1)}) custom-call(bf16[64,1152]{1,0:T(8,128)(2,1)} %img_hbm.1, bf16[512,1152]{1,0:T(8,128)(2,1)} %cap_hbm.1, s32[64,128]{1,0:T(8,128)} %bitcast.1, f32[1]{0:T(128)S(6)} %copy.11.nlm_ref, f32[1]{0:T(128)S(6)} %copy.12.bias_ref), custom_call_target="tpu_custom_call" | custom-call | tf_op jit(solution)/shard_map/pallas_call | solution.py:402
  75.0 0.7 copy.9
  75.7 1.4 %copy.10 = f32[512,1152]{1,0:T(8,128)} copy(f32[512,1152]{1,0:T(8,128)S(1)} %get-tuple-element.3) | data formatting | bytes 4718592

commit v4 on v3

--- a/solution.py
+++ b/solution.py
@@ -11,25 +11,26 @@
 BF16 = jnp.bfloat16
 
 
-YPOS = 2
+SETUP = ("p", 2)
+YPOS = 4
 ORDER = (
-    ("sx", 0), ("t", 0), ("t", 1), ("p", 0), ("p", 1), ("t", 2), ("t", 3), ("t", 4), ("t", 5), ("t", 6), ("p", 2),
-    ("f", 0, 1), ("f", 0, 3), ("rx", 0), ("p", 3), ("ry", 3), ("sx", 3), ("f", 1, 3), ("f", 1, 1), ("f", 2, 1),
-    ("f", 2, 3), ("ry", 1), ("sx", 1), ("f", 3, 3), ("f", 0, 2), ("p", 4), ("f", 1, 2), ("f", 3, 1), ("rx", 3),
-    ("p", 5), ("f", 2, 2), ("f", 3, 2), ("p", 6), ("f", 4, 1), ("rx", 1), ("f", 4, 3), ("p", 7), ("f", 5, 1),
-    ("f", 5, 3), ("p", 8), ("f", 6, 1), ("f", 6, 3), ("sx", 2), ("A", 0, 0), ("A", 1, 0), ("A", 2, 0), ("A", 3, 0),
-    ("f", 4, 2), ("f", 7, 3), ("A", 4, 0), ("f", 7, 1), ("f", 5, 2), ("f", 8, 1), ("A", 5, 0), ("f", 8, 3), ("rx", 2),
-    ("A", 5, 1), ("A", 1, 1), ("A", 2, 3), ("A", 2, 1), ("A", 4, 3), ("A", 0, 3), ("A", 3, 1), ("A", 3, 3),
-    ("A", 1, 3), ("A", 5, 3), ("f", 6, 2), ("A", 0, 1), ("A", 4, 1), ("f", 7, 2), ("f", 8, 2), ("A", 6, 0),
-    ("A", 6, 1), ("A", 6, 3), ("A", 7, 3), ("A", 8, 3), ("A", 7, 1), ("A", 8, 1), ("A", 7, 0), ("A", 8, 0),
-    ("C", 1, 0), ("A", 8, 2), ("B", 8), ("A", 6, 2), ("A", 4, 2), ("A", 1, 2), ("A", 2, 2), ("A", 0, 2), ("A", 7, 2),
-    ("B", 7), ("A", 3, 2), ("A", 5, 2), ("zf", 8), ("B", 6), ("C", 2, 0), ("zf", 7), ("B", 5), ("C", 0, 1), ("zf", 6),
-    ("C", 2, 1), ("zl", 8), ("C", 0, 0), ("zf", 5), ("B", 4), ("zl", 7), ("B", 3), ("C", 3, 0), ("xl", 2), ("zl", 6),
-    ("C", 3, 1), ("zf", 4), ("zz", 8), ("zf", 3), ("zl", 5), ("B", 2), ("B", 1), ("zz", 7), ("xl", 0), ("C", 1, 1),
-    ("xl", 1), ("zz", 6), ("zf", 2), ("B", 0), ("e", 6), ("xl", 3), ("xz", 2), ("zl", 4), ("zl", 3), ("zf", 1),
-    ("e", 5), ("zf", 0), ("zz", 5), ("e", 4), ("zl", 2), ("xz", 1), ("yz", 1), ("zz", 4), ("zz", 3), ("e", 3),
-    ("xz", 3), ("zl", 1), ("yz", 0), ("zl", 0), ("xz", 0), ("zz", 2), ("e", 2), ("zz", 1), ("zz", 0), ("end",),
-    ("e", 1), ("e", 0),
+    ("sx", 0), ("t", 0), ("t", 1), ("p", 0), ("p", 1), ("t", 2), ("t", 3), ("t", 4), ("p", 2), ("f", 0, 1),
+    ("f", 0, 3), ("rx", 0), ("p", 3), ("f", 1, 3), ("f", 1, 1), ("sx", 3), ("ry", 3), ("t", 5), ("t", 6), ("p", 4),
+    ("f", 2, 1), ("f", 2, 3), ("p", 5), ("f", 0, 2), ("f", 3, 3), ("f", 1, 2), ("f", 3, 1), ("rx", 3), ("ry", 1),
+    ("sx", 1), ("f", 4, 1), ("f", 4, 3), ("p", 6), ("f", 2, 2), ("f", 5, 3), ("sx", 2), ("A", 0, 0), ("f", 3, 2),
+    ("A", 2, 0), ("f", 5, 1), ("A", 1, 0), ("p", 7), ("A", 3, 0), ("f", 4, 2), ("f", 6, 3), ("p", 8), ("A", 4, 0),
+    ("f", 5, 2), ("f", 6, 1), ("rx", 1), ("A", 5, 0), ("f", 7, 1), ("f", 7, 3), ("rx", 2), ("A", 1, 1), ("A", 4, 1),
+    ("A", 3, 1), ("A", 0, 1), ("A", 5, 1), ("A", 2, 1), ("f", 8, 1), ("f", 8, 3), ("A", 2, 3), ("A", 3, 3),
+    ("A", 1, 3), ("A", 0, 3), ("f", 6, 2), ("A", 4, 3), ("A", 5, 3), ("f", 7, 2), ("A", 6, 0), ("A", 6, 1),
+    ("A", 6, 3), ("A", 7, 1), ("A", 7, 3), ("f", 8, 2), ("A", 7, 0), ("A", 0, 2), ("A", 7, 2), ("B", 7), ("A", 8, 1),
+    ("A", 2, 2), ("A", 8, 2), ("A", 8, 0), ("A", 8, 3), ("B", 8), ("C", 1, 0), ("A", 4, 2), ("A", 3, 2), ("zf", 7),
+    ("A", 1, 2), ("A", 6, 2), ("B", 6), ("zf", 8), ("A", 5, 2), ("C", 2, 0), ("B", 5), ("C", 0, 1), ("zf", 6),
+    ("zl", 7), ("B", 2), ("C", 2, 1), ("zl", 8), ("zf", 5), ("B", 1), ("B", 4), ("B", 3), ("zl", 6), ("C", 3, 0),
+    ("xl", 2), ("C", 3, 1), ("zz", 8), ("zz", 7), ("zf", 4), ("C", 1, 1), ("xl", 0), ("xl", 1), ("zl", 5), ("zf", 3),
+    ("B", 0), ("zf", 2), ("zz", 6), ("C", 0, 0), ("e", 6), ("zl", 4), ("xz", 2), ("xl", 3), ("zf", 0), ("e", 5),
+    ("zz", 5), ("e", 4), ("zl", 3), ("zl", 2), ("zf", 1), ("xz", 1), ("yz", 1), ("zz", 4), ("e", 3), ("zl", 0),
+    ("xz", 3), ("yz", 0), ("zz", 3), ("zz", 2), ("zl", 1), ("xz", 0), ("e", 2), ("zz", 0), ("end",), ("e", 1),
+    ("zz", 1), ("e", 0),
 )
 
 
@@ -90,6 +91,7 @@
     cols = 4 * n_img
     rows = 8 * R
     half = n_img // 2
+    two = 2 * n_img
     blk = lax.axis_index("blk")
     grp = lax.axis_index("group")
     core, x, ylo = lax.rem(blk, 2), lax.rem(lax.div(blk, 2), 4), lax.div(blk, 8)
@@ -123,44 +125,50 @@
     loads[0].wait()
     imgbuf[pl.ds(0, n_img), :] = normalize(img_ref[...])[0].astype(BF16)
     loads[1].wait()
-    for t in range(nt):
+    def make_tail(t):
         tsend[t] = normalize(cap_ref[pl.ds(kept + t * R, R), :])[0].astype(BF16)
 
-    loads[2].wait()
-    two = 2 * n_img
-    image_row = lax.broadcasted_iota(jnp.int32, (n_img, two), 0)
-    image_lane = lax.broadcasted_iota(jnp.int32, (n_img, two), 1)
-
-    def running_ends(device, lanes):
-        number = device[0] * 8 + device[1]
-        counts = cnt_ref[pl.ds(lax.div(number, 2), 1), :].astype(F32)
-        local = image_lane - lax.rem(number, 2) * n_img
-        lower = jnp.where(jnp.logical_and(local >= 0, local <= image_row), counts, 0.0)
-        return jnp.dot(lower.astype(BF16), jnp.ones((two, lanes), BF16), preferred_element_type=F32)
-
-    own_ends = running_ends((blk, grp), width)
-    tots[0:1, :] = own_ends[n_img - 1 :, :]
-    log_row = jnp.full((1, rows), nlm_ref[0], F32)
-    consts[0:1, :] = jnp.exp(log_row) * 0.5
-    consts[1:2, :] = jnp.full((1, rows), bias_ref[0] * 0.5, F32)
-
-    own_part = own_ends[:, :rows]
-    pair_ends = running_ends(partner, rows)
-    total_row = own_part[n_img - 1 :, :]
-    lane = lax.broadcasted_iota(jnp.int32, (1, rows), 1)
-    for k in range(nk):
-        position = (lane + k * R).astype(F32)
-        own_index = jnp.sum(jnp.where(own_part <= position, 1.0, 0.0), axis=0, keepdims=True)
-        slot = position - total_row + float(kept)
-        pair_index = jnp.sum(jnp.where(pair_ends <= slot, 1.0, 0.0), axis=0, keepdims=True)
-        column = jnp.where(position < total_row, own_index, float(place[1] * n_img) + pair_index)
-        midx[k : k + 1, :] = jnp.where(lane < R, column, -1.0).astype(jnp.int32)
-
+    def make_head(k):
+        capbuf[pl.ds(k * rows, R), :] = normalize(cap_ref[pl.ds(k * R, R), :])[0].astype(BF16)
+
+    for i in range(2):
+        make_tail(i)
+        make_head(i)
     pl.semaphore_wait(barrier, 7)
 
     def before_total(first):
         position = lax.broadcasted_iota(jnp.int32, (R, width), 0) + first
         return position.astype(F32) < tots[0:1, :]
+
+    def setup():
+        loads[2].wait()
+        image_row = lax.broadcasted_iota(jnp.int32, (n_img, two), 0)
+        image_lane = lax.broadcasted_iota(jnp.int32, (n_img, two), 1)
+
+        def running_ends(device, lanes):
+            number = device[0] * 8 + device[1]
+            counts = cnt_ref[pl.ds(lax.div(number, 2), 1), :].astype(F32)
+            local = image_lane - lax.rem(number, 2) * n_img
+            lower = jnp.where(jnp.logical_and(local >= 0, local <= image_row), counts, 0.0)
+            return jnp.dot(lower.astype(BF16), jnp.ones((two, lanes), BF16), preferred_element_type=F32)
+
+        own_ends = running_ends((blk, grp), width)
+        tots[0:1, :] = own_ends[n_img - 1 :, :]
+        log_row = jnp.full((1, rows), nlm_ref[0], F32)
+        consts[0:1, :] = jnp.exp(log_row) * 0.5
+        consts[1:2, :] = jnp.full((1, rows), bias_ref[0] * 0.5, F32)
+
+        own_part = own_ends[:, :rows]
+        pair_ends = running_ends(partner, rows)
+        total_row = own_part[n_img - 1 :, :]
+        lane = lax.broadcasted_iota(jnp.int32, (1, rows), 1)
+        for k in range(nk):
+            position = (lane + k * R).astype(F32)
+            own_index = jnp.sum(jnp.where(own_part <= position, 1.0, 0.0), axis=0, keepdims=True)
+            slot = position - total_row + float(kept)
+            pair_index = jnp.sum(jnp.where(pair_ends <= slot, 1.0, 0.0), axis=0, keepdims=True)
+            column = jnp.where(position < total_row, own_index, float(place[1] * n_img) + pair_index)
+            midx[k : k + 1, :] = jnp.where(lane < R, column, -1.0).astype(jnp.int32)
 
     def send_x(yr):
         if yr == 2:
@@ -182,14 +190,16 @@
         copies.send(("y2", yr), img_at(0, yr, first, half), img_at(0, 2, first, half), dev(0, step))
 
     def tail(t):
+        if t >= 2:
+            make_tail(t)
         copies.send(("t", t), tsend.at[t], trecv.at[pl.ds(t * R, R)], partner)
         if t == YPOS - 1:
             copies.send(("y", 1), img_at(0, 0), img_at(0, 1), partner)
             copies.send(("y", 3), img_at(0, 0), img_at(0, 3), dev(0, -near))
 
     def pack(k):
-        block = normalize(cap_ref[pl.ds(k * R, R), :])[0]
         if k >= 2:
+            block = normalize(cap_ref[pl.ds(k * R, R), :])[0]
             copies.wait("t", k - 2)
             count = (k - 1) * R
             row = (lax.broadcasted_iota(jnp.int32, (R, count), 0) + k * R).astype(F32)
@@ -197,7 +207,7 @@
             pick = jnp.where(row - tots[0:1, :count] == lane, 1.0, 0.0).astype(BF16)
             moved = jnp.dot(pick, trecv[pl.ds(0, count), :], preferred_element_type=F32)
             block = jnp.where(before_total(k * R), block, moved)
-        capbuf[pl.ds(k * rows, R), :] = block.astype(BF16)
+            capbuf[pl.ds(k * rows, R), :] = block.astype(BF16)
         copies.send(("zp", k), cap_at(k, 0, 0), cap_at(k, 0, 1), dev(0, 0, 1))
         copies.send(("zm", k), cap_at(k, 0, 0), cap_at(k, 0, 3), dev(0, 0, -1))
         copies.send(("s", 0, k), cap_at(k, 0, 0), cap_at(k, 1, 0), sibling)
@@ -353,6 +363,8 @@
         zf=z_first, zl=z_late, zz=z_last, e=tail_last, xl=x_late, xz=x_last, yz=y_late, end=finish,
     )
     for kind, *numbers in ORDER:
+        if (kind, *numbers) == SETUP:
+            setup()
         actions[kind](*numbers)
     copies.drain()
 

time: 77.3 us -> 76.3 us (0.987)
  Pallas kernels: 73.1 us -> 72.1 us
    pallas_call x1, Pallas kernels: 73.1 us -> 72.1 us  [shards(): pl.pallas_call(kernel, out_shape=(pltpu.VMEM((n_img, width), F32), pltpu....]
where the time goes in v4:
time: 76.3 us; the launch traced here: 76.1 us
  Pallas kernels  72.1 us (94%)
  local copies, waits for them, and re-layouts  2.12 us (3%)
  between operations  1.93 us (3%)
    pallas_call x1, Pallas kernels, shards(): pl.pallas_call(kernel, out_shape=(pltpu.VMEM((n_img, width), F32), pltpu....  72.1 us
    unnamed x2, local copies, waits for them, and re-layouts  2.12 us

profile of v4, /device:TPU:1, one launch (start us, length us, event | category | flops | bytes accessed | tf_op | source)
XLA Modules:
  0.0 76.1 jit_solution(13316867209402511089)
XLA Ops:
  1.9 72.1 %shard_map.68 = (f32[64,1152]{1,0:T(8,128)S(1)}, f32[512,1152]{1,0:T(8,128)S(1)}) custom-call(bf16[64,1152]{1,0:T(8,128)(2,1)} %img_hbm.1, bf16[512,1152]{1,0:T(8,128)(2,1)} %cap_hbm.1, s32[64,128]{1,0:T(8,128)} %bitcast.1, f32[1]{0:T(128)S(6)} %copy.11.nlm_ref, f32[1]{0:T(128)S(6)} %copy.12.bias_ref), custom_call_target="tpu_custom_call" | custom-call | tf_op jit(solution)/shard_map/pallas_call | solution.py:414
  74.0 0.7 copy.9
  74.7 1.4 %copy.10 = f32[512,1152]{1,0:T(8,128)} copy(f32[512,1152]{1,0:T(8,128)S(1)} %get-tuple-element.3) | data formatting | bytes 4718592

commit v5 on v4

--- a/solution.py
+++ b/solution.py
@@ -14,23 +14,23 @@
 SETUP = ("p", 2)
 YPOS = 4
 ORDER = (
-    ("sx", 0), ("t", 0), ("t", 1), ("p", 0), ("p", 1), ("t", 2), ("t", 3), ("t", 4), ("p", 2), ("f", 0, 1),
-    ("f", 0, 3), ("rx", 0), ("p", 3), ("f", 1, 3), ("f", 1, 1), ("sx", 3), ("ry", 3), ("t", 5), ("t", 6), ("p", 4),
-    ("f", 2, 1), ("f", 2, 3), ("p", 5), ("f", 0, 2), ("f", 3, 3), ("f", 1, 2), ("f", 3, 1), ("rx", 3), ("ry", 1),
-    ("sx", 1), ("f", 4, 1), ("f", 4, 3), ("p", 6), ("f", 2, 2), ("f", 5, 3), ("sx", 2), ("A", 0, 0), ("f", 3, 2),
-    ("A", 2, 0), ("f", 5, 1), ("A", 1, 0), ("p", 7), ("A", 3, 0), ("f", 4, 2), ("f", 6, 3), ("p", 8), ("A", 4, 0),
-    ("f", 5, 2), ("f", 6, 1), ("rx", 1), ("A", 5, 0), ("f", 7, 1), ("f", 7, 3), ("rx", 2), ("A", 1, 1), ("A", 4, 1),
-    ("A", 3, 1), ("A", 0, 1), ("A", 5, 1), ("A", 2, 1), ("f", 8, 1), ("f", 8, 3), ("A", 2, 3), ("A", 3, 3),
-    ("A", 1, 3), ("A", 0, 3), ("f", 6, 2), ("A", 4, 3), ("A", 5, 3), ("f", 7, 2), ("A", 6, 0), ("A", 6, 1),
-    ("A", 6, 3), ("A", 7, 1), ("A", 7, 3), ("f", 8, 2), ("A", 7, 0), ("A", 0, 2), ("A", 7, 2), ("B", 7), ("A", 8, 1),
-    ("A", 2, 2), ("A", 8, 2), ("A", 8, 0), ("A", 8, 3), ("B", 8), ("C", 1, 0), ("A", 4, 2), ("A", 3, 2), ("zf", 7),
-    ("A", 1, 2), ("A", 6, 2), ("B", 6), ("zf", 8), ("A", 5, 2), ("C", 2, 0), ("B", 5), ("C", 0, 1), ("zf", 6),
-    ("zl", 7), ("B", 2), ("C", 2, 1), ("zl", 8), ("zf", 5), ("B", 1), ("B", 4), ("B", 3), ("zl", 6), ("C", 3, 0),
-    ("xl", 2), ("C", 3, 1), ("zz", 8), ("zz", 7), ("zf", 4), ("C", 1, 1), ("xl", 0), ("xl", 1), ("zl", 5), ("zf", 3),
-    ("B", 0), ("zf", 2), ("zz", 6), ("C", 0, 0), ("e", 6), ("zl", 4), ("xz", 2), ("xl", 3), ("zf", 0), ("e", 5),
-    ("zz", 5), ("e", 4), ("zl", 3), ("zl", 2), ("zf", 1), ("xz", 1), ("yz", 1), ("zz", 4), ("e", 3), ("zl", 0),
-    ("xz", 3), ("yz", 0), ("zz", 3), ("zz", 2), ("zl", 1), ("xz", 0), ("e", 2), ("zz", 0), ("end",), ("e", 1),
-    ("zz", 1), ("e", 0),
+    ("sx", 0), ("t", 0), ("t", 1), ("p", 0), ("p", 1), ("t", 2), ("t", 3), ("t", 4), ("p", 2), ("f", 0, 3),
+    ("f", 0, 1), ("rx", 0), ("p", 3), ("f", 1, 3), ("f", 1, 1), ("sx", 3), ("ry", 3), ("t", 5), ("t", 6), ("p", 4),
+    ("f", 2, 1), ("f", 2, 3), ("p", 5), ("f", 0, 2), ("f", 3, 3), ("f", 1, 2), ("f", 3, 1), ("gy", 3, 0), ("rx", 3),
+    ("ry", 1), ("sx", 1), ("f", 4, 3), ("f", 4, 1), ("p", 6), ("gy", 1, 0), ("f", 2, 2), ("f", 5, 3), ("A", 0, 0),
+    ("A", 2, 0), ("f", 3, 2), ("f", 5, 1), ("A", 1, 0), ("p", 7), ("gy", 1, 1), ("A", 3, 0), ("f", 4, 2), ("f", 6, 3),
+    ("p", 8), ("A", 4, 0), ("f", 5, 2), ("f", 6, 1), ("gy", 3, 1), ("rx", 1), ("A", 5, 0), ("f", 7, 1), ("f", 7, 3),
+    ("rx", 2), ("A", 1, 1), ("A", 3, 1), ("A", 4, 1), ("A", 0, 1), ("A", 2, 1), ("A", 5, 1), ("f", 8, 1), ("f", 8, 3),
+    ("f", 6, 2), ("A", 3, 3), ("A", 2, 3), ("A", 4, 3), ("A", 1, 3), ("f", 7, 2), ("A", 0, 3), ("A", 5, 3),
+    ("A", 6, 0), ("A", 6, 1), ("A", 6, 3), ("A", 7, 3), ("A", 7, 1), ("A", 7, 0), ("f", 8, 2), ("A", 0, 2),
+    ("A", 7, 2), ("B", 7), ("A", 8, 1), ("A", 8, 0), ("A", 8, 2), ("A", 2, 2), ("A", 8, 3), ("B", 8), ("C", 1, 0),
+    ("zf", 7), ("A", 4, 2), ("A", 6, 2), ("B", 6), ("zf", 8), ("A", 3, 2), ("A", 1, 2), ("A", 5, 2), ("C", 2, 0),
+    ("B", 5), ("zf", 6), ("C", 2, 1), ("zl", 7), ("B", 3), ("C", 3, 0), ("zl", 8), ("zf", 5), ("B", 4), ("C", 1, 1),
+    ("zl", 6), ("zf", 3), ("xl", 2), ("B", 1), ("C", 3, 1), ("zf", 4), ("zz", 8), ("zz", 7), ("B", 2), ("zl", 5),
+    ("zf", 1), ("B", 0), ("xl", 1), ("xl", 0), ("zl", 3), ("C", 0, 1), ("zz", 6), ("zf", 2), ("C", 0, 0), ("e", 6),
+    ("xz", 2), ("xl", 3), ("zz", 5), ("e", 5), ("zl", 4), ("zf", 0), ("zl", 1), ("e", 4), ("xz", 1), ("yz", 1),
+    ("zl", 2), ("e", 3), ("zz", 4), ("zz", 3), ("xz", 3), ("yz", 0), ("zl", 0), ("zz", 1), ("xz", 0), ("zz", 2),
+    ("e", 2), ("zz", 0), ("e", 1), ("end",), ("e", 0),
 )
 
 
@@ -171,23 +171,32 @@
             midx[k : k + 1, :] = jnp.where(lane < R, column, -1.0).astype(jnp.int32)
 
     def send_x(yr):
-        if yr == 2:
-            copies.wait("y2", 1)
-            copies.wait("y2", 3)
-        elif yr:
+        if yr:
             copies.wait("y", yr)
         copies.send(("xp", yr), img_at(0, yr), img_at(1, yr), dev(1))
         copies.send(("xm", yr), img_at(0, yr), img_at(3, yr), dev(-1))
 
+    def wait_image(xr, yr):
+        if yr == 2 and xr != 2:
+            for part in range(2):
+                copies.wait(*(("g", xr, part) if xr else ("y2", 2 * part + 1)))
+        elif xr or yr:
+            copies.wait(("y", "xp", "xr", "xm")[xr], yr)
+
     def relay_x(yr):
-        kind, xr = ("xp", 1) if yr % 2 == 0 else ("xm", 3)
-        copies.wait(kind, yr)
+        xr = 1 if yr % 2 == 0 else 3
+        wait_image(xr, yr)
         copies.send(("xr", yr), img_at(xr, yr), img_at(2, yr), dev(sign(yr)))
 
     def relay_y(yr):
         copies.wait("y", yr)
         first, step = (0, -near) if yr == 1 else (half, near)
         copies.send(("y2", yr), img_at(0, yr, first, half), img_at(0, 2, first, half), dev(0, step))
+
+    def across_y(xr, part):
+        yr, first, step = ((3, 0, near), (1, half, -near))[part]
+        wait_image(xr, yr)
+        copies.send(("g", xr, part), img_at(xr, yr, first, half), img_at(xr, 2, first, half), dev(0, step))
 
     def tail(t):
         if t >= 2:
@@ -221,12 +230,8 @@
     def weights(k, xr):
         for zr in range(4):
             copies.wait("s", zr, k)
-        if xr == 0:
-            for name in (("y", 1), ("y", 3), ("y2", 1), ("y2", 3)):
-                copies.wait(*name)
-        else:
-            for yr in range(4):
-                copies.wait(("", "xp", "xr", "xm")[xr], yr)
+        for yr in range(4):
+            wait_image(xr, yr)
         products = lax.dot_general(
             imgbuf[pl.ds(xr * cols, cols), :],
             capbuf[pl.ds(k * rows, rows), :],
@@ -243,12 +248,13 @@
         wt[pl.ds(xr * cols, cols), pl.ds(k * rows, rows)] = half_tanh.astype(BF16)
 
     def caption_part(k):
-        part = lax.dot_general(
-            wt[:, pl.ds(k * rows, rows)], imgbuf[...], (((0,), (0,)), ((), ())), preferred_element_type=F32
-        )
-        pown[k] = part[: 4 * R, :]
-        d2ds[k] = part[4 * R :, :].astype(BF16)
+        def of(side):
+            block = wt[:, pl.ds(k * rows + side * 4 * R, 4 * R)]
+            return lax.dot_general(block, imgbuf[...], (((0,), (0,)), ((), ())), preferred_element_type=F32)
+
+        d2ds[k] = of(1).astype(BF16)
         copies.send(("d", k), d2ds.at[k], d2dr.at[k], sibling)
+        pown[k] = of(0)
 
     def z_first(k):
         copies.wait("d", k)
@@ -359,7 +365,7 @@
         iout[...] = (sums - unit * jnp.sum(unit * sums, axis=1, keepdims=True)) * inverse
 
     actions = dict(
-        sx=send_x, rx=relay_x, ry=relay_y, t=tail, p=pack, f=forward, A=weights, B=caption_part, C=image_part,
+        sx=send_x, gy=across_y, rx=relay_x, ry=relay_y, t=tail, p=pack, f=forward, A=weights, B=caption_part, C=image_part,
         zf=z_first, zl=z_late, zz=z_last, e=tail_last, xl=x_late, xz=x_last, yz=y_late, end=finish,
     )
     for kind, *numbers in ORDER:

time: 76.3 us -> 77.5 us (1.016)
  Pallas kernels: 72.1 us -> 73.2 us
    pallas_call x1, Pallas kernels: 72.1 us -> 73.2 us  [shards(): pl.pallas_call(kernel, out_shape=(pltpu.VMEM((n_img, width), F32), pltpu....]
where the time goes in v5:
time: 77.5 us; the launch traced here: 77.2 us
  Pallas kernels  73.2 us (94%)
  local copies, waits for them, and re-layouts  2.12 us (3%)
  between operations  1.93 us (2%)
    pallas_call x1, Pallas kernels, shards(): pl.pallas_call(kernel, out_shape=(pltpu.VMEM((n_img, width), F32), pltpu....  73.2 us
    unnamed x2, local copies, waits for them, and re-layouts  2.12 us

profile of v5, /device:TPU:1, one launch (start us, length us, event | category | flops | bytes accessed | tf_op | source)
XLA Modules:
  0.0 77.2 jit_solution(9689163174604448983)
XLA Ops:
  1.9 73.2 %shard_map.68 = (f32[64,1152]{1,0:T(8,128)S(1)}, f32[512,1152]{1,0:T(8,128)S(1)}) custom-call(bf16[64,1152]{1,0:T(8,128)(2,1)} %img_hbm.1, bf16[512,1152]{1,0:T(8,128)(2,1)} %cap_hbm.1, s32[64,128]{1,0:T(8,128)} %bitcast.1, f32[1]{0:T(128)S(6)} %copy.11.nlm_ref, f32[1]{0:T(128)S(6)} %copy.12.bias_ref), custom_call_target="tpu_custom_call" | custom-call | tf_op jit(solution)/shard_map/pallas_call | solution.py:420
  75.1 0.7 copy.9
  75.8 1.4 %copy.10 = f32[512,1152]{1,0:T(8,128)} copy(f32[512,1152]{1,0:T(8,128)S(1)} %get-tuple-element.3) | data formatting | bytes 4718592
